TPU v7x, 32 devices: a whole 2x2x4 slice. The times are simulated.
32 devices in a mesh: dp: 2 (over x), col: 4 (over z), row: 4 (over y, core).
Axes of the slice: x: 2, y: 2, z: 4, core: 2. Of those that a mesh axis runs over, the one named last changes fastest.
Arguments:
- x_norm: bfloat16 [1024, 4096], P(('dp', 'row'), 'col'), parts along dimension 0
- grad_y: bfloat16 [1024, 4096], P(('dp', 'row'), 'col'), parts along dimension 0
- w_gate: bfloat16 [4096, 10240], P('row', 'col')
- w_up: bfloat16 [4096, 10240], P('row', 'col')
- w_out: bfloat16 [10240, 4096], P('row', 'col')
Outputs:
- output 1: bfloat16 [1024, 4096], P(('dp', 'row'), 'col'), parts along dimension 0
- output 2: float32 [8192, 10240], P(('dp', 'row'), 'col'), parts along dimension 0
- output 3: float32 [8192, 10240], P(('dp', 'row'), 'col'), parts along dimension 0
- output 4: float32 [20480, 4096], P(('dp', 'row'), 'col'), parts along dimension 0
There are 2 independent parts. A program takes and returns all parts, laid end to end along the dimension named above; an argument that names none is the same for every part.
All inputs are finite; a program needn't handle non-finite values.
Results may differ from a plain program's by a relative error of at most 0.011032.
Values are sent between devices in bfloat16 or wider.
A program may use at most 1 GiB of HBM per device.

v0:
```python
import math
import jax
import jax.numpy as jnp
from jax import lax
from jax.sharding import PartitionSpec as P

GELU_SCALE = math.sqrt(2.0 / math.pi)
ROW_DIMS = (((1,), (1,)), ((), ()))
COL_DIMS = (((0,), (0,)), ((), ()))


def gelu_pair(pre_act):
    pre_f32 = pre_act.astype(jnp.float32)
    inner_arg = GELU_SCALE * (pre_f32 + 0.044715 * pre_f32 * pre_f32 * pre_f32)
    tanh_val = jnp.tanh(inner_arg)
    gelu_val = 0.5 * pre_f32 * (1.0 + tanh_val)
    gelu_der = 0.5 * (1.0 + tanh_val) + 0.5 * pre_f32 * (1.0 - tanh_val * tanh_val) * GELU_SCALE * (1.0 + 3.0 * 0.044715 * pre_f32 * pre_f32)
    return gelu_val, gelu_der


def solution(mesh):
    act_spec = P(("dp", "row"), "col")
    weight_spec = P("row", "col")

    def block_backward(x_blk, gy_blk, gate_blk, up_blk, out_blk):
        x_band = lax.all_gather(x_blk, "col", axis=1, tiled=True)
        gate_band = lax.all_gather(gate_blk, "row", axis=0, tiled=True)
        up_band = lax.all_gather(up_blk, "row", axis=0, tiled=True)
        out_band = lax.all_gather(out_blk, "row", axis=0, tiled=True)
        pre_gate = jnp.dot(x_band, gate_band, preferred_element_type=jnp.float32).astype(jnp.bfloat16)
        pre_up = jnp.dot(x_band, up_band, preferred_element_type=jnp.float32).astype(jnp.bfloat16)
        gelu_val, gelu_der = gelu_pair(pre_gate)
        up_f32 = pre_up.astype(jnp.float32)
        hidden = (gelu_val * up_f32).astype(jnp.bfloat16)
        grad_h_part = lax.dot_general(gy_blk, out_band, ROW_DIMS, preferred_element_type=jnp.float32)
        grad_h = lax.psum_scatter(grad_h_part, "col", scatter_dimension=1, tiled=True)
        hidden_band = lax.all_gather(hidden, "col", axis=1, tiled=True)
        dw_out_part = lax.dot_general(hidden_band, gy_blk, COL_DIMS, preferred_element_type=jnp.float32)
        dw_out = lax.psum_scatter(dw_out_part, "row", scatter_dimension=0, tiled=True)
        grad_gate = (grad_h * up_f32 * gelu_der).astype(jnp.bfloat16)
        grad_up = (grad_h * gelu_val).astype(jnp.bfloat16)
        grad_x_part = lax.dot_general(grad_gate, gate_band, ROW_DIMS, preferred_element_type=jnp.float32) + lax.dot_general(grad_up, up_band, ROW_DIMS, preferred_element_type=jnp.float32)
        grad_x = lax.psum_scatter(grad_x_part, "col", scatter_dimension=1, tiled=True).astype(jnp.bfloat16)
        dw_gate = lax.psum_scatter(lax.dot_general(x_band, grad_gate, COL_DIMS, preferred_element_type=jnp.float32), "row", scatter_dimension=0, tiled=True)
        dw_up = lax.psum_scatter(lax.dot_general(x_band, grad_up, COL_DIMS, preferred_element_type=jnp.float32), "row", scatter_dimension=0, tiled=True)
        return grad_x, dw_gate, dw_up, dw_out

    return jax.shard_map(block_backward, mesh=mesh, in_specs=(act_spec, act_spec, weight_spec, weight_spec, weight_spec), out_specs=(act_spec, act_spec, act_spec, act_spec), check_vma=False)
```

profile of v0, /device:TPU:0, one launch (start us, length us, event | category | flops | bytes accessed | tf_op | source)
XLA Modules:
  0.0 1510.0 jit_solution(13900176983351949858)
XLA Ops:
  7.2 0.7 all-gather.6.cloned.1.call-update
  7.9 0.0 all-gather.8.cloned.1.call-start
  8.0 0.7 all-gather.8.cloned.1.call-update
  8.7 0.0 all-gather.12.cloned.1.call-start
  8.7 0.7 all-gather.12.cloned.1.call-update
  9.4 0.5 all-gather.10.cloned.1.call-update
  10.0 0.0 reduce-scatter.6.cloned.1.call-start
  10.0 134.8 %all-gather.6.cloned.1.call-done = bf16[10240,1024]{1,0:T(8,128)(2,1)} async-done(((bf16[2560,1024]{1,0:T(8,128)(2,1)}), bf16[10240,1024]{1,0:T(8,128)(2,1)}) %all-gather.6.cloned.1.call-update) | async-done | bytes 20971536 | tf_op jit(solution)/shard_map/all_gather | solution.py:29
  144.8 13.4 fusion.9
  158.2 0.0 all-gather.14.cloned.1.call-start
  158.2 16.1 %all-gather.8.cloned.1.call-done = bf16[128,4096]{1,0:T(8,128)(2,1)} async-done(((bf16[128,1024]{1,0:T(8,128)(2,1)}), bf16[128,4096]{1,0:T(8,128)(2,1)}) %all-gather.8.cloned.1.call-update) | async-done | bytes 1048592 | tf_op jit(solution)/shard_map/all_gather | solution.py:26
  174.3 133.4 %all-gather.12.cloned.1.call-done = bf16[4096,2560]{1,0:T(8,128)(2,1)} async-done(((bf16[1024,2560]{1,0:T(8,128)(2,1)}), bf16[4096,2560]{1,0:T(8,128)(2,1)}) %all-gather.12.cloned.1.call-update) | async-done | bytes 20971536 | tf_op jit(solution)/shard_map/all_gather | solution.py:27
  307.7 11.2 fusion
  319.0 122.7 %all-gather.10.cloned.1.call-done = bf16[4096,2560]{1,0:T(8,128)(2,1)} async-done(((bf16[1024,2560]{1,0:T(8,128)(2,1)}), bf16[4096,2560]{1,0:T(8,128)(2,1)}) %all-gather.10.cloned.1.call-update) | async-done | bytes 20971536 | tf_op jit(solution)/shard_map/all_gather | solution.py:28
  441.6 96.3 %reduce-scatter.6.cloned.1.call-done = f32[128,2560]{1,0:T(8,128)} async-done(((f32[128,10240]{1,0:T(8,128)}), f32[128,2560]{1,0:T(8,128)}) %reduce-scatter.6.cloned.1.call-update) | async-done | bytes 1310736 | tf_op jit(solution)/shard_map/reduce_scatter | solution.py:36
  537.9 12.2 multiply_convert_fusion
  550.1 0.2 reduce-scatter.8.cloned.1.call-start
  550.4 10.9 fusion.10
  561.2 12.7 convolution_add_fusion
  573.9 0.0 reduce-scatter.10.cloned.1.call-start
  573.9 16.3 %convolution_bitcast_fusion.1 = f32[4096,2560]{0,1:T(8,128)} fusion(bf16[128,2560]{1,0:T(8,128)(2,1)S(1)} %get-tuple-element.9, bf16[128,4096]{1,0:T(8,128)(2,1)S(1)} %copy-done.1), kind=kOutput, calls=%fused_computation.1 | convolution fusion | flops 2684354560 | bytes 43646976 | tf_op jit(solution)/shard_map/dot_general | solution.py:44
  590.3 0.0 reduce-scatter.12.cloned.1.call-start
  590.4 16.2 %convolution_bitcast_fusion = f32[4096,2560]{0,1:T(8,128)} fusion(bf16[128,2560]{1,0:T(8,128)(2,1)S(1)} %get-tuple-element.10, bf16[128,4096]{1,0:T(8,128)(2,1)S(1)} %copy-done.1), kind=kOutput, calls=%fused_computation | convolution fusion | flops 2684354560 | bytes 43646976 | tf_op jit(solution)/shard_map/dot_general | solution.py:45
  606.6 0.3 reduce-scatter.14.cloned.1.call-start
  606.9 18.1 %fusion.11 = f32[10240,1024]{1,0:T(8,128)} fusion(bf16[128,10240]{1,0:T(8,128)(2,1)} %all-gather.14.cloned.1.call-done, bf16[128,1024]{1,0:T(8,128)(2,1)S(1)} %copy-done), kind=kOutput, calls=%fused_computation.21 | convolution fusion | flops 2684354560 | bytes 44826624 | tf_op jit(solution)/shard_map/dot_general | solution.py:38
  625.0 25.7 %reduce-scatter.8.cloned.1.call-done = f32[128,1024]{1,0:T(8,128)} async-done(((f32[128,4096]{1,0:T(8,128)}), f32[128,1024]{1,0:T(8,128)}) %reduce-scatter.8.cloned.1.call-update) | async-done | bytes 524304 | tf_op jit(solution)/shard_map/reduce_scatter | solution.py:43
  650.7 1.8 convert_element_type.30
  652.5 281.5 %reduce-scatter.10.cloned.1.call-done = f32[1024,2560]{0,1:T(8,128)} async-done(((f32[4096,2560]{0,1:T(8,128)}), f32[1024,2560]{0,1:T(8,128)}) %reduce-scatter.10.cloned.1.call-update) | async-done | bytes 10485776 | tf_op jit(solution)/shard_map/reduce_scatter | solution.py:44
  934.0 11.4 copy.9
  945.4 273.0 %reduce-scatter.12.cloned.1.call-done = f32[1024,2560]{0,1:T(8,128)} async-done(((f32[4096,2560]{0,1:T(8,128)}), f32[1024,2560]{0,1:T(8,128)}) %reduce-scatter.12.cloned.1.call-update) | async-done | bytes 10485776 | tf_op jit(solution)/shard_map/reduce_scatter | solution.py:45
  1218.4 11.4 copy.10
  1229.8 273.4 %reduce-scatter.14.cloned.1.call-done = f32[2560,1024]{1,0:T(8,128)} async-done(((f32[10240,1024]{1,0:T(8,128)}), f32[2560,1024]{1,0:T(8,128)}) %reduce-scatter.14.cloned.1.call-update) | async-done | bytes 10485776 | tf_op jit(solution)/shard_map/reduce_scatter | solution.py:39
  (13 shorter events, 0.2 us)
Async XLA Ops:
  7.2 137.6 %copy-start = (bf16[128,1024]{1,0:T(8,128)(2,1)S(1)}, bf16[128,1024]{1,0:T(8,128)(2,1)}, u32[]{:S(2)}) copy-start(bf16[128,1024]{1,0:T(8,128)(2,1)} %param.6) | copy-start | bytes 786436
  7.2 137.6 %all-gather.6.cloned.1.call-start = ((), (), s32[]{:S(2)}) async-start(), calls=%async_computation.5 | async-start | bytes 26214400 | tf_op jit(solution)/shard_map/all_gather | solution.py:29
  7.9 166.4 %all-gather.8.cloned.1.call-start = ((), (), s32[]{:S(2)}) async-start(), calls=%async_computation.7 | async-start | bytes 1310720 | tf_op jit(solution)/shard_map/all_gather | solution.py:26
  8.7 299.0 %all-gather.12.cloned.1.call-start = ((), (), s32[]{:S(2)}) async-start(), calls=%async_computation.9 | async-start | bytes 26214400 | tf_op jit(solution)/shard_map/all_gather | solution.py:27
  9.4 432.2 %all-gather.10.cloned.1.call-start = ((), (), s32[]{:S(2)}) async-start(), calls=%async_computation.8 | async-start | bytes 26214400 | tf_op jit(solution)/shard_map/all_gather | solution.py:28
  10.0 527.9 %reduce-scatter.6.cloned.1.call-start = ((), (), s32[]{:S(2)}) async-start(), calls=%async_computation.6 | async-start | bytes 6553600 | tf_op jit(solution)/shard_map/reduce_scatter | solution.py:36
  158.2 448.7 %all-gather.14.cloned.1.call-start = ((), (), s32[]{:S(2)}) async-start(), calls=%async_computation.13 | async-start | bytes 3276800 | tf_op jit(solution)/shard_map/all_gather | solution.py:37
  174.3 363.6 %copy-start.1 = (bf16[128,4096]{1,0:T(8,128)(2,1)S(1)}, bf16[128,4096]{1,0:T(8,128)(2,1)}, u32[]{:S(2)}) copy-start(bf16[128,4096]{1,0:T(8,128)(2,1)} %all-gather.8.cloned.1.call-done) | copy-start | bytes 3145732
  550.1 100.6 %reduce-scatter.8.cloned.1.call-start = ((), (), s32[]{:S(2)}) async-start(), calls=%async_computation.10 | async-start | bytes 2621440 | tf_op jit(solution)/shard_map/reduce_scatter | solution.py:43
  573.9 360.1 %reduce-scatter.10.cloned.1.call-start = ((), (), s32[]{:S(2)}) async-start(), calls=%async_computation.11 | async-start | bytes 52428800 | tf_op jit(solution)/shard_map/reduce_scatter | solution.py:44
  590.3 628.1 %reduce-scatter.12.cloned.1.call-start = ((), (), s32[]{:S(2)}) async-start(), calls=%async_computation.12 | async-start | bytes 52428800 | tf_op jit(solution)/shard_map/reduce_scatter | solution.py:45
  606.6 896.6 %reduce-scatter.14.cloned.1.call-start = ((), (), s32[]{:S(2)}) async-start(), calls=%async_computation.14 | async-start | bytes 52428800 | tf_op jit(solution)/shard_map/reduce_scatter | solution.py:39
Sparse Core Ops, SparseCore 0:
  9.6 135.1 all-gather.5
  146.4 27.8 all-gather.7
  175.9 131.7 all-gather.11
  309.1 132.4 all-gather.9
  444.3 93.5 reduce-scatter.5
  550.2 54.7 all-gather.13
  607.9 42.7 reduce-scatter.7
  653.3 280.6 reduce-scatter.9
  936.6 281.7 reduce-scatter.11
  1221.4 281.7 reduce-scatter.13
where the time goes:
time: 1510 us
  waiting for transfers between devices  1360 us (90%)
  matrix products  111 us (7%)
  local copies, waits for them, and re-layouts  22.8 us (2%)
    reduce_scatter x1, waiting for transfers between devices, block_backward(): lax.psum_scatter(lax.dot_general(x_band, grad_gate, COL_DIMS, preferred_e...  281 us
    reduce_scatter x1, waiting for transfers between devices, block_backward(): lax.psum_scatter(dw_out_part, 'row', scatter_dimension=0, tiled=True)  273 us
    reduce_scatter x1, waiting for transfers between devices, block_backward(): lax.psum_scatter(lax.dot_general(x_band, grad_up, COL_DIMS, preferred_ele...  273 us
    all_gather x1, waiting for transfers between devices, block_backward(): out_band = lax.all_gather(out_blk, 'row', axis=0, tiled=True)  135 us
    all_gather x1, waiting for transfers between devices, block_backward(): gate_band = lax.all_gather(gate_blk, 'row', axis=0, tiled=True)  133 us
    all_gather x1, waiting for transfers between devices, block_backward(): up_band = lax.all_gather(up_blk, 'row', axis=0, tiled=True)  123 us
    reduce_scatter x1, waiting for transfers between devices, block_backward(): lax.psum_scatter(grad_h_part, 'col', scatter_dimension=1, tiled=True)  96.3 us
  transfers between devices with their start and end apart: 10, of which 9 were waited for; matrix products, arithmetic and copies ran while one was open for 8% of the time, Pallas kernels for 0%

commit v1 on v0

v1 whole, which is shorter than its diff:
```python
import math
import jax
import jax.numpy as jnp
from jax import lax
from jax.sharding import PartitionSpec as P

GELU_SCALE = math.sqrt(2.0 / math.pi)
ROW_DIMS = (((1,), (1,)), ((), ()))
COL_DIMS = (((0,), (0,)), ((), ()))


def gelu_pair(pre_act):
    pre_f32 = pre_act.astype(jnp.float32)
    inner_arg = GELU_SCALE * (pre_f32 + 0.044715 * pre_f32 * pre_f32 * pre_f32)
    tanh_val = jnp.tanh(inner_arg)
    gelu_val = 0.5 * pre_f32 * (1.0 + tanh_val)
    gelu_der = 0.5 * (1.0 + tanh_val) + 0.5 * pre_f32 * (1.0 - tanh_val * tanh_val) * GELU_SCALE * (1.0 + 3.0 * 0.044715 * pre_f32 * pre_f32)
    return gelu_val, gelu_der


def solution(mesh):
    act_spec = P(("dp", "row"), "col")
    weight_spec = P("row", "col")
    n = mesh.shape["row"]
    swap = [(c * n + r, r * n + c) for c in range(n) for r in range(n)]

    def transpose_blocks(v):
        return lax.ppermute(v, ("col", "row"), swap)

    def block_backward(x_blk, gy_blk, gate_blk, up_blk, out_blk):
        x_all = lax.all_gather(transpose_blocks(x_blk), "col", axis=0, tiled=True)
        gy_all = lax.all_gather(gy_blk, "row", axis=0, tiled=True)
        gate_part = jnp.dot(x_all, gate_blk, preferred_element_type=jnp.float32)
        up_part = jnp.dot(x_all, up_blk, preferred_element_type=jnp.float32)
        pre_gate = lax.psum_scatter(gate_part, "row", scatter_dimension=0, tiled=True).astype(jnp.bfloat16)
        pre_up = lax.psum_scatter(up_part, "row", scatter_dimension=0, tiled=True).astype(jnp.bfloat16)
        grad_h_part = lax.dot_general(gy_all, out_blk, ROW_DIMS, preferred_element_type=jnp.float32)
        grad_h = lax.psum_scatter(grad_h_part, "col", scatter_dimension=0, tiled=True)
        pre_gate = transpose_blocks(pre_gate)
        pre_up = transpose_blocks(pre_up)
        gelu_val, gelu_der = gelu_pair(pre_gate)
        up_f32 = pre_up.astype(jnp.float32)
        hidden = (gelu_val * up_f32).astype(jnp.bfloat16)
        hidden_all = lax.all_gather(hidden, "col", axis=0, tiled=True)
        grad_gate = transpose_blocks((grad_h * up_f32 * gelu_der).astype(jnp.bfloat16))
        grad_up = transpose_blocks((grad_h * gelu_val).astype(jnp.bfloat16))
        grad_gate = lax.all_gather(grad_gate, "row", axis=0, tiled=True)
        grad_up = lax.all_gather(grad_up, "row", axis=0, tiled=True)
        grad_x_part = lax.dot_general(grad_gate, gate_blk, ROW_DIMS, preferred_element_type=jnp.float32) + lax.dot_general(grad_up, up_blk, ROW_DIMS, preferred_element_type=jnp.float32)
        grad_x = transpose_blocks(lax.psum_scatter(grad_x_part, "col", scatter_dimension=0, tiled=True).astype(jnp.bfloat16))
        dw_gate = lax.dot_general(x_all, grad_gate, COL_DIMS, preferred_element_type=jnp.float32)
        dw_up = lax.dot_general(x_all, grad_up, COL_DIMS, preferred_element_type=jnp.float32)
        dw_out = lax.dot_general(hidden_all, gy_all, COL_DIMS, preferred_element_type=jnp.float32)
        return grad_x, dw_gate, dw_up, dw_out

    return jax.shard_map(block_backward, mesh=mesh, in_specs=(act_spec, act_spec, weight_spec, weight_spec, weight_spec), out_specs=(act_spec, act_spec, act_spec, act_spec), check_vma=False)
```

time: 1510 us -> 546 us (0.36)
  waiting for transfers between devices: 1360 us -> 430 us
  matrix products: 111 us -> 60 us
    reduce_scatter x5 -> x4, waiting for transfers between devices: 950 us -> 243 us  [the longest x1 113 us: block_backward(): lax.psum_scatter(grad_h_part, 'col', scatter_dimension=0, tiled=True)]
    all_gather x5, waiting for transfers between devices: 407 us -> 185 us  [the longest x1 65.1 us: block_backward(): grad_up = lax.all_gather(grad_up, 'row', axis=0, tiled=True)]
    dot_general x8, matrix products: 111 us -> 60 us  [the longest x1 9.11 us: block_backward(): lax.dot_general(hidden_all, gy_all, COL_DIMS, preferred_element_type=jnp....]
  transfers between devices with their start and end apart: 10 -> 15, of which waited for: 9 -> 9; matrix products, arithmetic and copies ran while one was open for 8% -> 16% of each run, Pallas kernels for 0% -> 0%
where the time goes in v1:
time: 546 us; the launch traced here: 543 us
  waiting for transfers between devices  430 us (79%)
  matrix products  60 us (11%)
  local copies, waits for them, and re-layouts  27 us (5%)
  between operations  14 us (3%)
  other arithmetic  7.14 us (1%)
  starting transfers between devices  5.63 us (1%)
    reduce_scatter x1, waiting for transfers between devices, block_backward(): lax.psum_scatter(grad_h_part, 'col', scatter_dimension=0, tiled=True)  113 us
    all_gather x1, waiting for transfers between devices, block_backward(): grad_up = lax.all_gather(grad_up, 'row', axis=0, tiled=True)  65.1 us
    reduce_scatter x1, waiting for transfers between devices, block_backward(): lax.psum_scatter(gate_part, 'row', scatter_dimension=0, tiled=True)  53.7 us
    all_gather x1, waiting for transfers between devices, block_backward(): hidden_all = lax.all_gather(hidden, 'col', axis=0, tiled=True)  48.7 us
    reduce_scatter x1, waiting for transfers between devices, block_backward(): lax.psum_scatter(up_part, 'row', scatter_dimension=0, tiled=True)  45.3 us
    all_gather x1, waiting for transfers between devices, block_backward(): x_all = lax.all_gather(transpose_blocks(x_blk), 'col', axis=0, tiled=True)  43.6 us
    reduce_scatter x1, waiting for transfers between devices, block_backward(): lax.psum_scatter(grad_x_part, 'col', scatter_dimension=0, tiled=True)  30.9 us
    unnamed x15, local copies, waits for them, and re-layouts  27 us
  transfers between devices with their start and end apart: 15, of which 9 were waited for; matrix products, arithmetic and copies ran while one was open for 16% of the time, Pallas kernels for 0%

profile of v1, /device:TPU:0, one launch (start us, length us, event | category | flops | bytes accessed | tf_op | source)
XLA Modules:
  0.0 543.4 jit_solution(1027754090523068579)
XLA Ops:
  7.2 1.6 collective-permute-start
  8.8 0.7 copy-done.2
  10.3 43.6 %all-gather.8.cloned.1.call-done = bf16[512,1024]{1,0:T(8,128)(2,1)} async-done(((bf16[128,1024]{1,0:T(8,128)(2,1)}), bf16[512,1024]{1,0:T(8,128)(2,1)}) %all-gather.8.cloned.1.call-update) | async-done | bytes 1048592 | tf_op jit(solution)/shard_map/all_gather | solution.py:31
  54.0 8.1 %fusion.12 = f32[512,2560]{1,0:T(8,128)} fusion(bf16[512,1024]{1,0:T(8,128)(2,1)} %all-gather.8.cloned.1.call-done, bf16[1024,2560]{1,0:T(8,128)(2,1)} %param.8), kind=kOutput, calls=%fused_computation.25 | convolution fusion | flops 2684354560 | bytes 11534336 | tf_op jit(solution)/shard_map/dot_general | solution.py:34
  62.1 1.1 copy-done.4
  63.3 7.0 %fusion.13 = f32[512,2560]{1,0:T(8,128)} fusion(bf16[512,1024]{1,0:T(8,128)(2,1)S(1)} %copy-done.4, bf16[1024,2560]{1,0:T(8,128)(2,1)} %param.7), kind=kOutput, calls=%fused_computation.26 | convolution fusion | flops 2684354560 | bytes 11534336 | tf_op jit(solution)/shard_map/dot_general | solution.py:33
  70.4 1.1 all-gather.6.cloned.1.call-done
  71.4 8.1 %fusion.11 = f32[512,2560]{1,0:T(8,128)} fusion(bf16[512,1024]{1,0:T(8,128)(2,1)} %all-gather.6.cloned.1.call-done, bf16[2560,1024]{1,0:T(8,128)(2,1)} %param.9), kind=kOutput, calls=%fused_computation.24 | convolution fusion | flops 2684354560 | bytes 11534336 | tf_op jit(solution)/shard_map/dot_general | solution.py:37
  79.6 45.3 %reduce-scatter.7.cloned.1.call-done = f32[128,2560]{1,0:T(8,128)} async-done(((f32[512,2560]{1,0:T(8,128)}), f32[128,2560]{1,0:T(8,128)}) %reduce-scatter.7.cloned.1.call-update) | async-done | bytes 1310736 | tf_op jit(solution)/shard_map/reduce_scatter | solution.py:36
  124.9 1.4 convert_element_type.24
  126.3 0.7 collective-permute-start.1
  127.0 53.7 %reduce-scatter.9.cloned.1.call-done = f32[128,2560]{1,0:T(8,128)} async-done(((f32[512,2560]{1,0:T(8,128)}), f32[128,2560]{1,0:T(8,128)}) %reduce-scatter.9.cloned.1.call-update) | async-done | bytes 1310736 | tf_op jit(solution)/shard_map/reduce_scatter | solution.py:35
  180.8 1.4 convert_element_type.26
  182.1 0.7 collective-permute-start.2
  182.9 113.1 %reduce-scatter.5.cloned.1.call-done = f32[128,2560]{1,0:T(8,128)} async-done(((f32[512,2560]{1,0:T(8,128)}), f32[128,2560]{1,0:T(8,128)}) %reduce-scatter.5.cloned.1.call-update) | async-done | bytes 1310736 | tf_op jit(solution)/shard_map/reduce_scatter | solution.py:38
  296.0 3.3 fusion.6
  300.0 0.8 copy-done
  300.9 0.7 collective-permute-start.3
  301.6 0.8 copy-done.1
  303.5 65.1 %all-gather.12.cloned.1.call-done = bf16[512,2560]{1,0:T(8,128)(2,1)} async-done(((bf16[128,2560]{1,0:T(8,128)(2,1)}), bf16[512,2560]{1,0:T(8,128)(2,1)}) %all-gather.12.cloned.1.call-update) | async-done | bytes 2621456 | tf_op jit(solution)/shard_map/all_gather | solution.py:48
  368.6 5.7 %fusion.14 = f32[512,1024]{1,0:T(8,128)S(1)} fusion(bf16[512,2560]{1,0:T(8,128)(2,1)} %all-gather.12.cloned.1.call-done, bf16[1024,2560]{1,0:T(8,128)(2,1)} %param.8), kind=kOutput, calls=%fused_computation.27 | convolution fusion | flops 2684354560 | bytes 9961472 | tf_op jit(solution)/shard_map/dot_general | solution.py:49
  374.2 26.6 %all-gather.10.cloned.1.call-done = bf16[512,2560]{1,0:T(8,128)(2,1)} async-done(((bf16[128,2560]{1,0:T(8,128)(2,1)}), bf16[512,2560]{1,0:T(8,128)(2,1)}) %all-gather.10.cloned.1.call-update) | async-done | bytes 2621456 | tf_op jit(solution)/shard_map/all_gather | solution.py:47
  400.8 7.5 %convolution_add_fusion = f32[512,1024]{1,0:T(8,128)} fusion(f32[512,1024]{1,0:T(8,128)S(1)} %fusion.14, bf16[512,2560]{1,0:T(8,128)(2,1)} %all-gather.10.cloned.1.call-done, bf16[1024,2560]{1,0:T(8,128)(2,1)} %param.7), kind=kOutput, calls=%fused_computation.13 | convolution fusion | flops 2684878848 | bytes 12058624 | tf_op jit(solution)/shard_map/dot_general | solution.py:49
  408.3 48.7 %all-gather.14.cloned.1.call-done = bf16[512,2560]{1,0:T(8,128)(2,1)} async-done(((bf16[128,2560]{1,0:T(8,128)(2,1)}), bf16[512,2560]{1,0:T(8,128)(2,1)}) %all-gather.14.cloned.1.call-update) | async-done | bytes 2621456 | tf_op jit(solution)/shard_map/all_gather | solution.py:44
  457.0 9.1 %fusion.15 = f32[2560,1024]{1,0:T(8,128)} fusion(bf16[512,2560]{1,0:T(8,128)(2,1)} %all-gather.14.cloned.1.call-done, bf16[512,1024]{1,0:T(8,128)(2,1)} %all-gather.6.cloned.1.call-done), kind=kOutput, calls=%fused_computation.28 | convolution fusion | flops 2684354560 | bytes 14155776 | tf_op jit(solution)/shard_map/dot_general | solution.py:53
  466.2 5.7 %convolution_bitcast_fusion = f32[1024,2560]{0,1:T(8,128)} fusion(bf16[512,2560]{1,0:T(8,128)(2,1)S(1)} %copy-done.3, bf16[512,1024]{1,0:T(8,128)(2,1)S(1)} %copy-done.5), kind=kOutput, calls=%fused_computation | convolution fusion | flops 2684354560 | bytes 14155776 | tf_op jit(solution)/shard_map/dot_general | solution.py:52
  471.8 30.9 %reduce-scatter.11.cloned.1.call-done = f32[128,1024]{1,0:T(8,128)} async-done(((f32[512,1024]{1,0:T(8,128)}), f32[128,1024]{1,0:T(8,128)}) %reduce-scatter.11.cloned.1.call-update) | async-done | bytes 524304 | tf_op jit(solution)/shard_map/reduce_scatter | solution.py:50
  502.7 1.1 convert_element_type.30
  504.5 8.9 %convolution_bitcast_fusion.1 = f32[1024,2560]{0,1:T(8,128)} fusion(bf16[512,2560]{1,0:T(8,128)(2,1)} %all-gather.10.cloned.1.call-done, bf16[512,1024]{1,0:T(8,128)(2,1)} %all-gather.8.cloned.1.call-done), kind=kOutput, calls=%fused_computation.1 | convolution fusion | flops 2684354560 | bytes 14155776 | tf_op jit(solution)/shard_map/dot_general | solution.py:51
  513.4 11.4 %copy.10 = f32[1024,2560]{1,0:T(8,128)} copy(f32[1024,2560]{0,1:T(8,128)} %convolution_bitcast_fusion) | data formatting | bytes 20971520
  524.8 11.4 %copy.9 = f32[1024,2560]{1,0:T(8,128)} copy(f32[1024,2560]{0,1:T(8,128)} %convolution_bitcast_fusion.1) | data formatting | bytes 20971520
  536.2 0.7 copy.12
  (34 shorter events, 3.5 us)
Async XLA Ops:
  7.2 46.8 %all-gather.8.cloned.1.call-start = ((), (), s32[]{:S(2)}) async-start(), calls=%async_computation.6 | async-start | bytes 1310720 | tf_op jit(solution)/shard_map/all_gather | solution.py:31
  7.2 1.6 collective-permute-start
  8.8 0.7 copy-start.2
  9.5 61.9 %all-gather.6.cloned.1.call-start = ((), (), s32[]{:S(2)}) async-start(), calls=%async_computation.4 | async-start | bytes 1310720 | tf_op jit(solution)/shard_map/all_gather | solution.py:32
  10.3 114.6 %reduce-scatter.7.cloned.1.call-start = ((), (), s32[]{:S(2)}) async-start(), calls=%async_computation.7 | async-start | bytes 6553600 | tf_op jit(solution)/shard_map/reduce_scatter | solution.py:36
  62.0 1.2 copy-start.4
  62.1 118.7 %reduce-scatter.9.cloned.1.call-start = ((), (), s32[]{:S(2)}) async-start(), calls=%async_computation.8 | async-start | bytes 6553600 | tf_op jit(solution)/shard_map/reduce_scatter | solution.py:35
  70.3 225.6 %reduce-scatter.5.cloned.1.call-start = ((), (), s32[]{:S(2)}) async-start(), calls=%async_computation.5 | async-start | bytes 6553600 | tf_op jit(solution)/shard_map/reduce_scatter | solution.py:38
  79.6 289.0 %all-gather.12.cloned.1.call-start = ((), (), s32[]{:S(2)}) async-start(), calls=%async_computation.10 | async-start | bytes 3276800 | tf_op jit(solution)/shard_map/all_gather | solution.py:48
  126.3 169.6 %collective-permute-start.1 = (bf16[128,2560]{1,0:T(8,128)(2,1)S(1)}, bf16[128,2560]{1,0:T(8,128)(2,1)S(1)}, u32[]{:S(2)}, u32[]{:S(2)}) collective-permute-start(bf16[128,2560]{1,0:T(8,128)(2,1)S(1)} %convert_element_type.24), channel_id=1, source_target_pairs={{0,0},{1,4},{2,8},{3,12},{4,1},{5,5},{6,9},{7,13},{8,2},{9,6},{10,... | collective-permute-start | bytes 1966088 | tf_op jit(solution)/shard_map/ppermute | solution.py:28
  182.1 113.8 %collective-permute-start.2 = (bf16[128,2560]{1,0:T(8,128)(2,1)S(1)}, bf16[128,2560]{1,0:T(8,128)(2,1)S(1)}, u32[]{:S(2)}, u32[]{:S(2)}) collective-permute-start(bf16[128,2560]{1,0:T(8,128)(2,1)S(1)} %convert_element_type.26), channel_id=1, source_target_pairs={{0,0},{1,4},{2,8},{3,12},{4,1},{5,5},{6,9},{7,13},{8,2},{9,6},{10,... | collective-permute-start | bytes 1966088 | tf_op jit(solution)/shard_map/ppermute | solution.py:28
  299.3 0.7 collective-permute-start.4
  300.0 0.8 copy-start
  300.8 99.9 %all-gather.10.cloned.1.call-start = ((), (), s32[]{:S(2)}) async-start(), calls=%async_computation.9 | async-start | bytes 3276800 | tf_op jit(solution)/shard_map/all_gather | solution.py:47
  300.9 0.7 collective-permute-start.3
  301.6 0.8 copy-start.1
  302.5 154.6 %all-gather.14.cloned.1.call-start = ((), (), s32[]{:S(2)}) async-start(), calls=%async_computation.12 | async-start | bytes 3276800 | tf_op jit(solution)/shard_map/all_gather | solution.py:44
  303.2 199.5 %reduce-scatter.11.cloned.1.call-start = ((), (), s32[]{:S(2)}) async-start(), calls=%async_computation.11 | async-start | bytes 2621440 | tf_op jit(solution)/shard_map/reduce_scatter | solution.py:50
  408.3 57.8 %copy-start.3 = (bf16[512,2560]{1,0:T(8,128)(2,1)S(1)}, bf16[512,2560]{1,0:T(8,128)(2,1)}, u32[]{:S(2)}) copy-start(bf16[512,2560]{1,0:T(8,128)(2,1)} %all-gather.12.cloned.1.call-done) | copy-start | bytes 7864324
  457.0 9.1 %copy-start.5 = (bf16[512,1024]{1,0:T(8,128)(2,1)S(1)}, bf16[512,1024]{1,0:T(8,128)(2,1)}, u32[]{:S(2)}) copy-start(bf16[512,1024]{1,0:T(8,128)(2,1)} %all-gather.8.cloned.1.call-done) | copy-start | bytes 3145732
  503.8 32.4 %collective-permute-start.5 = (bf16[128,1024]{1,0:T(8,128)(2,1)S(1)}, bf16[128,1024]{1,0:T(8,128)(2,1)S(1)}, u32[]{:S(2)}, u32[]{:S(2)}) collective-permute-start(bf16[128,1024]{1,0:T(8,128)(2,1)S(1)} %convert_element_type.30), channel_id=1, source_target_pairs={{0,0},{1,4},{2,8},{3,12},{4,1},{5,5},{6,9},{7,13},{8,2},{9,6},{10,... | collective-permute-start | bytes 786440 | tf_op jit(solution)/shard_map/ppermute | solution.py:28
Sparse Core Ops, SparseCore 0:
  10.1 43.8 all-gather.7
  55.5 15.8 all-gather.5
  74.6 50.3 reduce-scatter.6
  127.9 52.7 reduce-scatter.8
  183.5 112.4 reduce-scatter.4
  301.0 67.5 all-gather.11
  370.7 30.0 all-gather.9
  402.9 54.0 all-gather.13
  459.9 42.7 reduce-scatter.10

commit v2 on v0

v2 whole, which is shorter than its diff:
```python
import math
import jax
import jax.numpy as jnp
from jax import lax
from jax.experimental import pallas as pl
from jax.experimental.pallas import tpu as pltpu
from jax.sharding import PartitionSpec as P

GELU_SCALE = math.sqrt(2.0 / math.pi)
F32, BF16 = jnp.float32, jnp.bfloat16
MESH = pl.DeviceIdType.MESH
ANY = pl.BlockSpec(memory_space=pl.ANY)
NT_DIMS = (((1,), (1,)), ((), ()))
TN_DIMS = (((0,), (0,)), ((), ()))
NCH = 4
N_CUT = ((0, 256), (256, 384))


def gelu_pair(pre_f32):
    inner_arg = GELU_SCALE * (pre_f32 + 0.044715 * pre_f32 * pre_f32 * pre_f32)
    tanh_val = jnp.tanh(inner_arg)
    gelu_val = 0.5 * pre_f32 * (1.0 + tanh_val)
    gelu_der = 0.5 * (1.0 + tanh_val) + 0.5 * pre_f32 * (1.0 - tanh_val * tanh_val) * GELU_SCALE * (1.0 + 3.0 * 0.044715 * pre_f32 * pre_f32)
    return gelu_val, gelu_der


class Slots:
    def __init__(self, ref, size):
        self.ref, self.size, self.names = ref, size, {}

    def __call__(self, *name):
        i = self.names.setdefault(name, len(self.names))
        assert i < self.size
        return self.ref.at[i]


N_SEND, N_RECV, N_LOCAL = 120, 120, 40


def comm_kernel(rows, dm, ff,
                x_hbm, gy_hbm, wg_hbm, wu_hbm, wo_hbm,
                xo, dyo, dbo, ho, dxo,
                XG, DY, WV, WP, WO, AS, AR, AO, DS, DR, DO, DB, HL, HP, DXS, DXA, DXB, DXF, DXR,
                send_ref, recv_ref, local_ref):
    fq = ff // 4
    cm = dm
    rb = rows // NCH
    tc = 4 * rb
    S, R, L = Slots(send_ref, N_SEND), Slots(recv_ref, N_RECV), Slots(local_ref, N_LOCAL)
    p, z, r = lax.axis_index("dp"), lax.axis_index("col"), lax.axis_index("row")
    y, k = r // 2, r % 2
    pr, c = z // 2, z % 2
    zm, zt = z + 1 - 2 * c, z + 2 - 4 * pr
    home = y == pr
    away = y != pr
    role = jnp.where(home, 0, 1)
    zeta = jnp.where(y == 0, z, 3 - z)
    zf, zb = z + 1 - 2 * y, z - 1 + 2 * y
    jA, jB = y, 1 - y
    ro, rp = 2 * (1 - y) + k, 2 * y + 1 - k

    def dev(z_=z, r_=r, p_=p):
        return {"dp": p_, "col": z_, "row": r_}

    pending = []

    def remote(src, dst, name, to):
        return pltpu.make_async_remote_copy(src_ref=src, dst_ref=dst, send_sem=S(*name), recv_sem=R(*name), device_id=to, device_id_type=MESH)

    def send(src, dst, name, to, cond=None, last=None):
        cp = remote(src, dst, name, to)
        if cond is None:
            cp.start()
        else:
            pl.when(cond)(cp.start)
        if last is not False:
            pending.append((cond if last is None else last, cp))
        return cp

    def got(dst, name, cond=None):
        cp = remote(dst, dst, name, dev(p_=1 - p))
        if cond is None:
            cp.wait_recv()
        else:
            pl.when(cond)(cp.wait_recv)

    def local(src, dst, *name):
        return pltpu.make_async_copy(src, dst, L(*name))

    barrier = pltpu.get_barrier_semaphore()
    peers = [dev(r_=rp), dev(r_=ro), dev(r_=2 * (1 - y) + 1 - k), dev(p_=1 - p), dev(z_=zt), dev(z_=zt + 1 - 2 * (zt % 2))]
    peers += [dev(z_=zm, r_=q) for q in range(4)]
    for peer in peers:
        pl.semaphore_signal(barrier, inc=1, device_id=peer, device_id_type=MESH)
    lx = local(x_hbm, XG.at[c, :, k, y], "x")
    pl.when(home)(lx.start)
    ldy = local(gy_hbm, DY.at[c, :, k, y], "dy")
    ldy.start()
    lw = []
    for m, w in enumerate((wg_hbm, wu_hbm)):
        for q in range(4):
            cp = local(w.at[:, pl.ds(q * fq, fq)], WV.at[m, q], "w", m, q)
            cp.start()
            lw.append(cp)

    def wo_cut(q, n, cols):
        off, ln = N_CUT[n]
        return wo_hbm.at[pl.ds(pl.multiple_of(q * fq + off, 128), ln), cols]

    def wo_slot(ro_, n, j, cols):
        off, ln = N_CUT[n]
        start, width = cols
        return WO.at[ro_, pl.ds(off, ln), pl.ds(pl.multiple_of(j * cm + start, 512), width)]

    half = cm // 2
    pcols = pl.ds(pl.multiple_of(p * half, 512), half)

    lwo = []
    for n in range(2):
        cp = local(wo_cut(r, n, pl.ds(0, cm)), wo_slot(role, n, c, (0, cm)), "wo", n)
        pl.when(k == c)(cp.start)
        lwo.append(cp)
    pl.semaphore_wait(barrier, len(peers))

    send(gy_hbm, DY.at[c, :, k, y], ("dyy",), dev(r_=ro))
    for th in range(2):
        ts = pl.ds(2 * th, 2)
        send(x_hbm.at[ts], XG.at[c, ts, k, y], ("xy", th), dev(r_=ro), away)

    def wo_near(n):
        send(wo_cut(rp, n, pl.ds(0, cm)), wo_slot(role, n, c, (0, cm)), ("wo", 0, n), dev(r_=rp), k == c)
        for k2 in range(2):
            q = 2 * (1 - y) + k2
            send(wo_cut(q, n, pcols), wo_slot(role, n, c, (p * half, half)), ("wo", 1, n, k2), dev(r_=q), k == c)

    def wo_far(n, cond):
        for dy_ in (1, 0):
            for k2 in range(2):
                q = 2 * (1 - y if dy_ else y) + k2
                send(wo_cut(q, n, pcols), wo_slot(role, n, c, (p * half, half)), ("wo", 2 + dy_, n, k2), dev(z_=zm, r_=q), cond, False)

    def wo_far_pending(n):
        for dy_ in (1, 0):
            for k2 in range(2):
                q = 2 * (1 - y if dy_ else y) + k2
                pending.append((k != c, remote(wo_cut(q, n, pcols), wo_slot(role, n, c, (p * half, half)), ("wo", 2 + dy_, n, k2), dev(z_=zm, r_=q))))

    far_away, far_home = jnp.logical_and(k != c, away), jnp.logical_and(k != c, home)
    for n in range(2):
        wo_near(n)
        wo_far_pending(n)
    wo_far(0, far_away)
    for m, w in enumerate((wg_hbm, wu_hbm)):
        for s in range(2):
            send(w.at[:, pl.ds(pl.multiple_of((1 - k + 2 * s) * fq, 128), fq)], WP.at[m, s], ("w", m, s), dev(r_=rp))

    def chain_start(name, A, B):
        send(A, A, (*name, "A"), dev(z_=zf), zeta == 0, zeta <= 2)
        send(B, B, (*name, "B"), dev(z_=zf), zeta == 1, jnp.logical_or(zeta == 1, zeta == 2))
        send(B, B, (*name, "b"), dev(z_=zb), zeta == 1)

    def chain_B(name, B):
        got(B, (*name, "b"), zeta == 0)
        got(B, (*name, "B"), zeta >= 2)
        send(B, B, (*name, "B"), dev(z_=zf), zeta == 2, False)

    def chain_A(name, A):
        got(A, (*name, "A"), zeta >= 1)
        send(A, A, (*name, "A"), dev(z_=zf), jnp.logical_or(zeta == 1, zeta == 2), False)

    ldy.wait()
    got(DY.at[c, :, k, 1 - y], ("dyy",))
    send(DY.at[c, :, k], DY.at[c, :, k], ("dyz",), dev(z_=zm))
    pl.when(home)(lx.wait)
    for th in range(2):
        ts = pl.ds(2 * th, 2)
        got(XG.at[c, ts, k, 1 - y], ("xy", th), home)
        chain_start(("x", th), XG.at[jA, ts, k], XG.at[jB, ts, k])
    send(DY.at[c, :, k], DY.at[c, :, k], ("dyd", 0), dev(r_=rp))
    wo_far(0, far_home)
    wo_far(1, far_home)

    def wo_pass(a, n):
        ro_ = jnp.where(role == 0, a % 2, 1 - a % 2)
        j = c if a == 1 else 1 - c
        mine = wo_slot(ro_, n, j, (p * half, half))
        got(mine, ("wo", a, n, 0), k == 0)
        got(mine, ("wo", a, n, 1), k == 1)
        send(mine, mine, ("wx", a, n), dev(p_=1 - p))

    def wo_have(a, n):
        ro_ = jnp.where(role == 0, a % 2, 1 - a % 2)
        j = c if a < 2 else 1 - c
        if a == 0:
            pl.when(k == c)(lwo[n].wait)
            got(wo_slot(ro_, n, j, (0, cm)), ("wo", 0, n), k != c)
        else:
            got(wo_slot(ro_, n, j, ((1 - p) * half, half)), ("wx", a, n))

    for th in range(2):
        ts = pl.ds(2 * th, 2)
        chain_B(("x", th), XG.at[jB, ts, k])
        send(XG.at[jB, ts, k], XG.at[jB, ts, k], ("xd", th, "B"), dev(r_=rp))
        wo_pass(1, th)
        wo_pass(2, th)
        chain_A(("x", th), XG.at[jA, ts, k])
        send(XG.at[jA, ts, k], XG.at[jA, ts, k], ("xd", th, "A"), dev(r_=rp))
        if th == 0:
            wo_far(1, far_away)
        wo_pass(3, th)
    got(DY.at[1 - c, :, k], ("dyz",))
    send(DY.at[1 - c, :, k], DY.at[1 - c, :, k], ("dyd", 1), dev(r_=rp))
    got(DY.at[c, :, 1 - k], ("dyd", 0))
    got(DY.at[1 - c, :, 1 - k], ("dyd", 1))

    def dh_part(ro_, n, dst):
        off, ln = N_CUT[n]
        acc = None
        for j in range(2):
            t = lax.dot_general(DY[j].reshape(NCH * tc, cm), WO[ro_, off:off + ln, j * cm:(j + 1) * cm], NT_DIMS, preferred_element_type=F32)
            acc = t if acc is None else acc + t
        dst[:, off:off + ln] = acc

    def dh_mirror(n):
        for a in range(4):
            cond = home if a % 2 else away
            pl.when(cond)(lambda a=a: wo_have(a, n))
        dh_part(1, n, DS)
        off, ln = N_CUT[n]
        send(DS.at[:, pl.ds(off, ln)], DR.at[:, pl.ds(off, ln)], ("dh", n), dev(z_=zt))

    def dh_own(n):
        for a in range(4):
            cond = away if a % 2 else home
            pl.when(cond)(lambda a=a: wo_have(a, n))
        dh_part(0, n, DO)

    def ab_part(s, t, m):
        own = jnp.dot(XG[k, t].reshape(tc, cm), WV[m, k + 2 * s], preferred_element_type=F32)
        return own + jnp.dot(XG[1 - k, t].reshape(tc, cm), WP[m, s], preferred_element_type=F32)

    def ab_mirror(t):
        for m in range(2):
            AS[t, m] = ab_part(1 - y, t, m)
        send(AS.at[t], AR.at[t], ("ab", t), dev(r_=ro))

    for cp in lw:
        cp.wait()
    for m in range(2):
        for s in range(2):
            got(WP.at[m, s], ("w", m, s))
    for th in range(2):
        ts = pl.ds(2 * th, 2)
        got(XG.at[jB, ts, 1 - k], ("xd", th, "B"))
        got(XG.at[jA, ts, 1 - k], ("xd", th, "A"))
        dh_mirror(th)
        ab_mirror(2 * th)
        ab_mirror(2 * th + 1)
    out_x = local(XG.at[k], xo, "xo")
    out_x.start()
    out_dy = local(DY.at[c], dyo, "dyo")
    out_dy.start()
    dh_own(0)
    dh_own(1)

    hs = jnp.where(home, c, 2)

    def finish(t):
        for m in range(2):
            AO[m] = ab_part(y, t, m)
        got(AR.at[t], ("ab", t))
        if t == 0:
            for n, (off, ln) in enumerate(N_CUT):
                got(DR.at[:, pl.ds(off, ln)], ("dh", n))

        def body(i, _):
            rs = pl.ds(pl.multiple_of(i * 16, 16), 16)
            rt = pl.ds(pl.multiple_of(t * tc + i * 16, 16), 16)
            a = (AO[0, rs] + AR[t, 0, rs]).astype(BF16).astype(F32)
            b = (AO[1, rs] + AR[t, 1, rs]).astype(BF16).astype(F32)
            g, gd = gelu_pair(a)
            dh = DO[rt] + DR[rt]
            HL[hs, y, t, rs] = (g * b).astype(BF16)
            DB[0, r, t, rs] = (dh * b * gd).astype(BF16)
            DB[1, r, t, rs] = (dh * g).astype(BF16)
            return 0

        lax.fori_loop(0, tc // 16, body, 0)

    def share(t):
        mine = DB.at[:, r, t]
        send(mine, mine, ("dby", t), dev(r_=ro))
        send(mine, mine, ("dbd", t), dev(r_=rp))
        send(HL.at[2, y, t], HL.at[c, y, t], ("hy", t), dev(r_=ro), away)

    def relay(t):
        theirs = DB.at[:, ro, t]
        got(theirs, ("dby", t))
        send(theirs, theirs, ("dbf", t), dev(r_=rp))
        got(HL.at[c, 1 - y, t], ("hy", t), home)
        chain_start(("h", t), HL.at[jA, :, t], HL.at[jB, :, t])

    def relay_h(t):
        chain_B(("h", t), HL.at[jB, :, t])
        chain_A(("h", t), HL.at[jA, :, t])
        send(HL.at[1 - k, :, t], HP.at[:, t], ("hd", t), dev(r_=rp))

    def dx_part(t):
        got(DB.at[:, rp, t], ("dbd", t))
        got(DB.at[:, 2 * (1 - y) + 1 - k, t], ("dbf", t))
        acc = None
        for m in range(2):
            for q in range(4):
                d = lax.dot_general(DB[m, q, t], WV[m, q], NT_DIMS, preferred_element_type=F32)
                acc = d if acc is None else acc + d
        DXS[t] = acc
        z2 = jnp.where(y == 0, 2, 1)
        send(DXS.at[t], DXA.at[t], ("dxa", t), dev(z_=z2), zeta == 3)
        send(DXS.at[t], DXA.at[t], ("dxm", t), dev(z_=r), jnp.logical_and(zeta < 2, z != r))

    def dx_mid(t):
        @pl.when(zeta == 2)
        def _():
            got(DXA.at[t], ("dxa", t))
            DXS[t] += DXA[t]
        send(DXS.at[t], DXB.at[t], ("dxb", t), dev(z_=r), zeta == 2)

    diag = z == r

    def dx_end(t):
        @pl.when(diag)
        def _():
            got(DXA.at[t], ("dxm", t))
            got(DXB.at[t], ("dxb", t))
            DXF[t] = (DXS[t] + DXA[t] + DXB[t]).astype(BF16).reshape(2, 2, rb, cm)
        for k2, y2, n in ((1 - k, y, 0), (k, 1 - y, 1), (1 - k, 1 - y, 2)):
            send(DXF.at[t, k2, y2], DXR.at[t], ("dxf", t, n), dev(r_=2 * y2 + k2), diag)

    def dx_take(t):
        @pl.when(diag)
        def _():
            DXR[t] = DXF[t, k, y]
        zk, zy = z % 2, z // 2
        got(DXR.at[t], ("dxf", t, 0), jnp.logical_and(zk != k, zy == y))
        got(DXR.at[t], ("dxf", t, 1), jnp.logical_and(zk == k, zy != y))
        got(DXR.at[t], ("dxf", t, 2), jnp.logical_and(zk != k, zy != y))

    for t in range(NCH + 3):
        if t < NCH:
            finish(t)
            share(t)
        if 0 <= t - 1 < NCH:
            relay(t - 1)
            dx_part(t - 1)
        if 0 <= t - 2 < NCH:
            dx_mid(t - 2)
            relay_h(t - 2)
        if 0 <= t - 3 < NCH:
            dx_end(t - 3)
    outs = [local(DB, dbo, "dbo"), local(HL.at[k], ho.at[:, k], "ho")]
    for cp in outs:
        cp.start()
    for t in range(NCH):
        got(HP.at[:, t], ("hd", t))
        dx_take(t)
    outs += [local(HP, ho.at[:, 1 - k], "hp"), local(DXR, dxo, "dxo")]
    for cp in outs[2:]:
        cp.start()
    for cond, cp in pending:
        if cond is None:
            cp.wait_send()
        else:
            pl.when(cond)(cp.wait_send)
    for cp in outs + [out_x, out_dy]:
        cp.wait()


def dw_kernel(x_hbm, dy_hbm, db_hbm, h_hbm, dx_hbm, dwg, dwu, dwo, dxo, X, XT, DY, DB, H, OA, OB, in_sem, out_sem):
    tok, fq = X.shape[0], DB.shape[-1]
    loads = [pltpu.make_async_copy(x_hbm, X, in_sem.at[0]), pltpu.make_async_copy(dy_hbm, DY, in_sem.at[1])]
    for m in range(2):
        for q in range(4):
            loads.append(pltpu.make_async_copy(db_hbm.at[m, q], DB.at[m, q], in_sem.at[2 + 4 * m + q]))
    for q in range(4):
        loads.append(pltpu.make_async_copy(h_hbm.at[q], H.at[q], in_sem.at[10 + q]))
    for cp in loads:
        cp.start()
    loads[0].wait()
    XT[...] = X[...].T
    outs = [None, None, None, None]
    for m, dst in ((0, dwg), (1, dwu)):
        for q in range(4):
            loads[2 + 4 * m + q].wait()
            slot = q % 2
            if outs[slot] is not None:
                outs[slot].wait()
            OA[slot] = jnp.dot(XT[...], DB[m, q], preferred_element_type=F32)
            outs[slot] = pltpu.make_async_copy(OA.at[slot], dst.at[:, pl.ds(q * fq, fq)], out_sem.at[slot])
            outs[slot].start()
    loads[1].wait()
    for q in range(4):
        loads[10 + q].wait()
        slot = q % 2
        if outs[2 + slot] is not None:
            outs[2 + slot].wait()
        OB[slot] = lax.dot_general(H[q], DY[...], TN_DIMS, preferred_element_type=F32)
        outs[2 + slot] = pltpu.make_async_copy(OB.at[slot], dwo.at[pl.ds(q * fq, fq)], out_sem.at[2 + slot])
        outs[2 + slot].start()
    for cp in outs:
        cp.wait()
    dxo[...] = dx_hbm[...]


def solution(mesh):
    act_spec = P(("dp", "row"), "col")
    weight_spec = P("row", "col")

    def block_backward(x_blk, gy_blk, gate_blk, up_blk, out_blk):
        rows, dm = x_blk.shape
        ff = gate_blk.shape[1]
        fq, rb = ff // 4, rows // NCH
        tc = 4 * rb
        tok = NCH * tc
        vm = pltpu.VMEM
        xg, dyg, dbg, hg, dxg = pl.pallas_call(
            lambda *refs: comm_kernel(rows, dm, ff, *refs),
            out_shape=[
                jax.ShapeDtypeStruct((NCH, 2, 2, rb, dm), BF16),
                jax.ShapeDtypeStruct((NCH, 2, 2, rb, dm), BF16),
                jax.ShapeDtypeStruct((2, 4, NCH, tc, fq), BF16),
                jax.ShapeDtypeStruct((2, 2, NCH, tc, fq), BF16),
                jax.ShapeDtypeStruct((NCH, rb, dm), BF16),
            ],
            in_specs=[ANY] * 5,
            out_specs=[ANY] * 5,
            scratch_shapes=[
                vm((2, NCH, 2, 2, rb, dm), BF16),
                vm((2, NCH, 2, 2, rb, dm), BF16),
                vm((2, 4, dm, fq), BF16),
                vm((2, 2, dm, fq), BF16),
                vm((2, fq, 2 * dm), BF16),
                vm((NCH, 2, tc, fq), F32),
                vm((NCH, 2, tc, fq), F32),
                vm((2, tc, fq), F32),
                vm((tok, fq), F32),
                vm((tok, fq), F32),
                vm((tok, fq), F32),
                vm((2, 4, NCH, tc, fq), BF16),
                vm((3, 2, NCH, tc, fq), BF16),
                vm((2, NCH, tc, fq), BF16),
                vm((NCH, tc, dm), F32),
                vm((NCH, tc, dm), F32),
                vm((NCH, tc, dm), F32),
                vm((NCH, 2, 2, rb, dm), BF16),
                vm((NCH, rb, dm), BF16),
                pltpu.SemaphoreType.DMA((N_SEND,)),
                pltpu.SemaphoreType.DMA((N_RECV,)),
                pltpu.SemaphoreType.DMA((N_LOCAL,)),
            ],
            compiler_params=pltpu.CompilerParams(collective_id=0, has_side_effects=True, vmem_limit_bytes=63 * 1024 * 1024),
            name="comm",
        )(x_blk.reshape(NCH, rb, dm), gy_blk.reshape(NCH, rb, dm), gate_blk, up_blk, out_blk)
        whole = pl.BlockSpec(memory_space=vm)
        dw_gate, dw_up, dw_out, grad_x = pl.pallas_call(
            dw_kernel,
            out_shape=[
                jax.ShapeDtypeStruct((dm, ff), F32),
                jax.ShapeDtypeStruct((dm, ff), F32),
                jax.ShapeDtypeStruct((ff, dm), F32),
                jax.ShapeDtypeStruct((rows, dm), BF16),
            ],
            in_specs=[ANY] * 4 + [whole],
            out_specs=[ANY] * 3 + [whole],
            scratch_shapes=[
                vm((tok, dm), BF16), vm((dm, tok), BF16), vm((tok, dm), BF16),
                vm((2, 4, tok, fq), BF16), vm((4, tok, fq), BF16),
                vm((2, dm, fq), F32), vm((2, fq, dm), F32),
                pltpu.SemaphoreType.DMA((14,)), pltpu.SemaphoreType.DMA((4,)),
            ],
            compiler_params=pltpu.CompilerParams(vmem_limit_bytes=60 * 1024 * 1024),
            name="dw",
        )(xg.reshape(tok, dm), dyg.reshape(tok, dm), dbg.reshape(2, 4, tok, fq), hg.reshape(4, tok, fq), dxg.reshape(rows, dm))
        return grad_x, dw_gate, dw_up, dw_out

    return jax.shard_map(block_backward, mesh=mesh, in_specs=(act_spec, act_spec, weight_spec, weight_spec, weight_spec), out_specs=(act_spec, act_spec, act_spec, act_spec), check_vma=False)
```

time: 1510 us -> 263 us (0.17)
  waiting for transfers between devices: 1360 us -> 0 us
  Pallas kernels: 0 us -> 262 us
  matrix products: 111 us -> 0 us
  local copies, waits for them, and re-layouts: 22.8 us -> 0 us
    reduce_scatter x5 -> x0, waiting for transfers between devices: 950 us -> none  [the longest x1 281 us: block_backward(): lax.psum_scatter(lax.dot_general(x_band, grad_gate, COL_DIMS, preferred_e...]
    all_gather x5 -> x0, waiting for transfers between devices: 407 us -> none  [the longest x1 135 us: block_backward(): out_band = lax.all_gather(out_blk, 'row', axis=0, tiled=True)]
    pallas_call x0 -> x2, Pallas kernels: none -> 262 us  [the longest x1 242 us: block_backward(): pl.pallas_call(lambda *refs: comm_kernel(rows, dm, ff, *refs), out_shape=...]
    dot_general x8 -> x0, matrix products: 111 us -> none  [the longest x1 18.1 us: block_backward(): lax.dot_general(hidden_band, gy_blk, COL_DIMS, preferred_element_type=jnp...]
    unnamed x6 -> x0, local copies, waits for them, and re-layouts: 22.8 us -> none
  transfers between devices with their start and end apart: 10 -> 0, of which waited for: 9 -> 0; matrix products, arithmetic and copies ran while one was open for 8% -> 0% of each run, Pallas kernels for 0% -> 0%
where the time goes in v2:
time: 263 us
  Pallas kernels  262 us (100%)
    pallas_call x1, Pallas kernels, block_backward(): pl.pallas_call(lambda *refs: comm_kernel(rows, dm, ff, *refs), out_shape=...  242 us
    pallas_call x1, Pallas kernels, block_backward(): pl.pallas_call(dw_kernel, out_shape=[jax.ShapeDtypeStruct((dm, ff), F32),...  19.8 us

profile of v2, /device:TPU:0, one launch (start us, length us, event | category | flops | bytes accessed | tf_op | source)
XLA Modules:
  0.0 262.9 jit_solution(12855285208125874880)
XLA Ops:
  0.6 242.2 %comm.1 = (bf16[4,2,2,32,1024]{4,3,2,1,0:T(8,128)(2,1)}, bf16[4,2,2,32,1024]{4,3,2,1,0:T(8,128)(2,1)}, bf16[2,4,4,128,640]{4,3,2,1,0:T(8,128)(2,1)}, bf16[2,2,4,...) custom-call(bf16[4,32,1024]{2,1,0:T(8,128)(2,1)} %bitcast.11, bf16[4,32,1024]{2,1,0:T(8,128)(2,1)} %bitcast.12, ...), custom_call_target="tpu_custom_call" | custom-call | tf_op jit(solution)/shard_map/comm/pallas_call | solution.py:425
  242.9 19.8 %dw.1 = (f32[1024,2560]{1,0:T(8,128)}, f32[1024,2560]{1,0:T(8,128)}, f32[2560,1024]{1,0:T(8,128)}, bf16[128,1024]{1,0:T(8,128)(2,1)}) custom-call(bf16[512,1024]{1,0:T(8,128)(2,1)} %bitcast.9, bf16[512,1024]{1,0:T(8,128)(2,1)} %bitcast.10, bf16[2,4,512,640]{3,2,1,0:T(8,128)(2,1)} %bitcast.7, bf16[4,512,640]{2,1,0:T(8,128)(2,1)} %bitcast.8, ...), custom_call_target="tpu_custom_call" | custom-call | tf_op jit(solution)/shard_map/dw/pallas_call | solution.py:464

commit v3 on v0

v3 whole, which is shorter than its diff:
```python
import math
import jax
import jax.numpy as jnp
from jax import lax
from jax.experimental import pallas as pl
from jax.experimental.pallas import tpu as pltpu
from jax.sharding import PartitionSpec as P

GELU_SCALE = math.sqrt(2.0 / math.pi)
F32, BF16 = jnp.float32, jnp.bfloat16
MESH = pl.DeviceIdType.MESH
ANY = pl.BlockSpec(memory_space=pl.ANY)
NT_DIMS = (((1,), (1,)), ((), ()))
TN_DIMS = (((0,), (0,)), ((), ()))
RBS = (48, 32, 32, 16)
NCH = len(RBS)
OFF = tuple(sum(RBS[:t]) for t in range(NCH))
X_CUT = ((0, 80), (80, 48))
N_CUT = ((0, 128), (128, 256), (384, 256))
NS = range(len(N_CUT))
N_SEND, N_RECV, N_LOCAL = 160, 160, 48


def gelu_pair(pre_f32):
    inner_arg = GELU_SCALE * (pre_f32 + 0.044715 * pre_f32 * pre_f32 * pre_f32)
    tanh_val = jnp.tanh(inner_arg)
    gelu_val = 0.5 * pre_f32 * (1.0 + tanh_val)
    gelu_der = 0.5 * (1.0 + tanh_val) + 0.5 * pre_f32 * (1.0 - tanh_val * tanh_val) * GELU_SCALE * (1.0 + 3.0 * 0.044715 * pre_f32 * pre_f32)
    return gelu_val, gelu_der


class Slots:
    def __init__(self, ref, size):
        self.ref, self.size, self.names = ref, size, {}

    def __call__(self, *name):
        i = self.names.setdefault(name, len(self.names))
        assert i < self.size
        return self.ref.at[i]


def comm_kernel(rows, dm, ff,
                x_hbm, gy_hbm, wg_hbm, wu_hbm, wo_hbm,
                xo, dyo, dbo, ho, dxo,
                XG, XR, DY, WV, WP, WO, WR, AS, AR, AO, DS, DR, DO, DB, HL, HP, DXS, DXA, DXM, DXF, DXR, XT,
                send_ref, recv_ref, local_ref):
    fq = ff // 4
    cm = dm
    S, R, L = Slots(send_ref, N_SEND), Slots(recv_ref, N_RECV), Slots(local_ref, N_LOCAL)
    p, z, r = lax.axis_index("dp"), lax.axis_index("col"), lax.axis_index("row")
    y, k = r // 2, r % 2
    pr, c = z // 2, z % 2
    zm, zt = z + 1 - 2 * c, z + 2 - 4 * pr
    home, away = y == pr, y != pr
    role = jnp.where(home, 0, 1)
    zeta = jnp.where(y == 0, z, 3 - z)
    zf, zb = z + 1 - 2 * y, z - 1 + 2 * y
    z2 = jnp.where(y == 0, 2, 1)
    jA, jB = y, 1 - y
    ro, rp = 2 * (1 - y) + k, 2 * y + 1 - k
    rx = 2 * (1 - y) + 1 - k
    diag = z == r

    def both(a, b):
        return jnp.logical_and(a, b)

    def dev(z_=z, r_=r, p_=p):
        return {"dp": p_, "col": z_, "row": r_}

    pending = []

    def remote(src, dst, name, to):
        return pltpu.make_async_remote_copy(src_ref=src, dst_ref=dst, send_sem=S(*name), recv_sem=R(*name), device_id=to, device_id_type=MESH)

    def send(src, dst, name, to, cond=None, last=None):
        cp = remote(src, dst, name, to)
        if cond is None:
            cp.start()
        else:
            pl.when(cond)(cp.start)
        if last is not False:
            pending.append((cond if last is None else None if last is True else last, cp))

    def got(dst, name, cond=None):
        cp = remote(dst, dst, name, dev(p_=1 - p))
        if cond is None:
            cp.wait_recv()
        else:
            pl.when(cond)(cp.wait_recv)

    def local(src, dst, *name):
        return pltpu.make_async_copy(src, dst, L(*name))

    barrier = pltpu.get_barrier_semaphore()
    peers = [dev(r_=rp), dev(r_=ro), dev(r_=rx), dev(p_=1 - p), dev(z_=zt), dev(z_=zt + 1 - 2 * (zt % 2))]
    peers += [dev(z_=zm, r_=q) for q in range(4)]
    for peer in peers:
        pl.semaphore_signal(barrier, inc=1, device_id=peer, device_id_type=MESH)

    @pl.when(jnp.logical_not(diag))
    def _():
        pl.semaphore_signal(barrier, inc=1, device_id=dev(z_=r, r_=z), device_id_type=MESH)

    lx = local(x_hbm, XG.at[c, k, y], "x")
    pl.when(home)(lx.start)
    ldy = local(gy_hbm, DY.at[c, k, y], "dy")
    ldy.start()
    lw = []
    for m, w in enumerate((wg_hbm, wu_hbm)):
        for q in range(4):
            cp = local(w.at[:, pl.ds(q * fq, fq)], WV.at[q, :, pl.ds(m * fq, fq)], "w", m, q)
            cp.start()
            lw.append(cp)

    def wo_cut(q, n, cols):
        off, ln = N_CUT[n]
        return wo_hbm.at[pl.ds(pl.multiple_of(q * fq + off, 128), ln), cols]

    def wo_slot(ro_, n, j, cols):
        off, ln = N_CUT[n]
        start, width = cols
        return WO.at[ro_, pl.ds(off, ln), pl.ds(pl.multiple_of(j * cm + start, 512), width)]

    half = cm // 2
    pcols = pl.ds(pl.multiple_of(p * half, 512), half)
    lwo = []
    for n in NS:
        cp = local(wo_cut(r, n, pl.ds(0, cm)), wo_slot(role, n, c, (0, cm)), "wo", n)
        pl.when(k == c)(cp.start)
        lwo.append(cp)
    pl.semaphore_wait(barrier, jnp.where(diag, len(peers), len(peers) + 1))

    def chunk(t):
        return pl.ds(OFF[t], RBS[t])

    def x_place(src_z, ts, cond):
        mine = src_z // 2 == y
        return ((XG.at[src_z % 2, k, y, ts], both(cond, mine)), (XR.at[src_z % 2, ts], both(cond, jnp.logical_not(mine))))

    def x_send(th):
        ts = pl.ds(*X_CUT[th])
        for name, to, cond in (("xr", z + 1, z < 3), ("xl", z - 1, z > 0)):
            for dst, ok in x_place(z, ts, cond):
                send(x_hbm.at[ts], dst, (name, th, 1), dev(z_=to), ok)
        send(x_hbm.at[ts], XG.at[c, k, y, ts], ("xy", th, 0), dev(r_=ro), away)

    def x_step(th, d, left):
        ts = pl.ds(*X_CUT[th])
        src_z, to = (z + d, z - 1) if left else (z - d, z + 1)
        here = src_z <= 3 if left else src_z >= 0
        more = both(here, to >= 0 if left else to <= 3)
        name = "xl" if left else "xr"
        for ref, ok in x_place(src_z, ts, here):
            got(ref, (name, th, d), ok)
            if d < 3:
                send(ref, ref, (name, th, d + 1), dev(z_=to), both(ok, more))
        ref, ok = x_place(src_z, ts, here)[1]
        same = src_z % 2 == c
        send(ref, XG.at[src_z % 2, k, y, ts], ("xy", th, 0), dev(r_=ro), both(ok, same))
        send(ref, XG.at[src_z % 2, k, y, ts], ("xy", th, 1), dev(r_=ro), both(ok, jnp.logical_not(same)))

    def x_give(th):
        ts = pl.ds(*X_CUT[th])
        if th == 0:
            pl.when(home)(lx.wait)
        got(XG.at[c, k, 1 - y, ts], ("xy", th, 0))
        got(XG.at[1 - c, k, 1 - y, ts], ("xy", th, 1))
        send(XG.at[:, k, :, ts], XG.at[:, k, :, ts], ("xd", th), dev(r_=rp))

    def x_take(th):
        got(XG.at[:, 1 - k, :, pl.ds(*X_CUT[th])], ("xd", th))

    def dy_pass():
        ldy.wait()
        got(DY.at[c, k, 1 - y], ("dyy",))
        send(DY.at[c, k], DY.at[c, k], ("dyz",), dev(z_=zm))
        send(DY.at[c, k], DY.at[c, k], ("dyd", 0), dev(r_=rp))

    def dy_give():
        got(DY.at[1 - c, k], ("dyz",))
        send(DY.at[1 - c, k], DY.at[1 - c, k], ("dyd", 1), dev(r_=rp))

    def dy_take():
        for i, j in enumerate((c, 1 - c)):
            got(DY.at[j, 1 - k], ("dyd", i))

    def wo_near(n, cond):
        send(wo_cut(rp, n, pl.ds(0, cm)), wo_slot(role, n, c, (0, cm)), ("wo", 0, n), dev(r_=rp), both(cond, k == c))
        for k2 in range(2):
            q = 2 * (1 - y) + k2
            send(wo_cut(q, n, pcols), wo_slot(role, n, c, (p * half, half)), ("wo", 1, n, k2), dev(r_=q), both(cond, k == c))

    def wo_far(n, cond):
        off, ln = N_CUT[n]
        for over in (0, 1):
            for k2 in range(2):
                q = 2 * (1 - y if over else y) + k2
                dst = WR.at[pl.ds(off, ln)] if over else wo_slot(role, n, c, (p * half, half))
                send(wo_cut(q, n, pcols), dst, ("wf" if over else "wo", 2, n, k2), dev(z_=zm, r_=2 * y + k2), both(cond, k != c))

    def wo_relay(n, cond):
        off, ln = N_CUT[n]
        for k2 in range(2):
            got(WR.at[pl.ds(off, ln)], ("wf", 2, n, k2), both(cond, k == k2))
        send(WR.at[pl.ds(off, ln)], wo_slot(role, n, 1 - c, (p * half, half)), ("wo", 3, n), dev(r_=ro), cond)

    def wo_role(a):
        return jnp.where(home, a % 2, 1 - a % 2)

    def wo_pass(a, n, cond):
        j = c if a == 1 else 1 - c
        mine = wo_slot(wo_role(a), n, j, (p * half, half))
        if a == 3:
            got(mine, ("wo", a, n), cond)
        else:
            for k2 in range(2):
                got(mine, ("wo", a, n, k2), both(cond, k == k2))
        send(mine, mine, ("wx", a, n), dev(p_=1 - p), cond)

    def wo_have(a, n, cond):
        j = c if a < 2 else 1 - c
        if a == 0:
            pl.when(both(cond, k == c))(lwo[n].wait)
            got(wo_slot(wo_role(a), n, j, (0, cm)), ("wo", 0, n), both(cond, k != c))
        else:
            got(wo_slot(wo_role(a), n, j, ((1 - p) * half, half)), ("wx", a, n), cond)

    def dh_part(ro_, n, dst):
        off, ln = N_CUT[n]
        acc = None
        for j in range(2):
            t = lax.dot_general(DY[j].reshape(4 * rows, cm), WO[ro_, off:off + ln, j * cm:(j + 1) * cm], NT_DIMS, preferred_element_type=F32)
            acc = t if acc is None else acc + t
        dst[:, :, off:off + ln] = acc.reshape(4, rows, ln)

    def dh_cols(n, t):
        off, ln = N_CUT[n]
        return slice(None), chunk(t) if n == NS[-1] else pl.ds(0, rows), pl.ds(off, ln)

    def dh_mirror(n):
        for a in range(4):
            wo_have(a, n, home if a % 2 else away)
        dh_part(1, n, DS)
        for t in range(NCH if n == NS[-1] else 1):
            send(DS.at[dh_cols(n, t)], DR.at[dh_cols(n, t)], ("dh", n, t), dev(z_=zt))

    def dh_own(n):
        for a in range(4):
            wo_have(a, n, away if a % 2 else home)
        dh_part(0, n, DO)

    def ab_part(s, t):
        tc = 4 * RBS[t]
        own = jnp.dot(XG[k, :, :, OFF[t]:OFF[t] + RBS[t]].reshape(tc, cm), WV[k + 2 * s], preferred_element_type=F32)
        other = jnp.dot(XG[1 - k, :, :, OFF[t]:OFF[t] + RBS[t]].reshape(tc, cm), WP[s], preferred_element_type=F32)
        return (own + other).reshape(4, RBS[t], 2 * fq)

    def ab_mirror(t, cond=None, last=True):
        def go():
            AS[:, OFF[t]:OFF[t] + RBS[t]] = ab_part(1 - y, t)

        go() if cond is None else pl.when(cond)(go)
        send(AS.at[:, chunk(t)], AR.at[:, chunk(t)], ("ab", t), dev(r_=ro), cond, last)

    def weights_here():
        for cp in lw:
            cp.wait()
        for m in range(2):
            for s in range(2):
                got(WP.at[s, :, pl.ds(m * fq, fq)], ("w", m, s))

    hs = jnp.where(home, c, 2)

    def row_blocks(t, fn):
        nb = RBS[t] // 16

        def body(i, _):
            fn(i // nb, pl.ds(pl.multiple_of(OFF[t] + i % nb * 16, 16), 16))
            return 0

        lax.fori_loop(0, 4 * nb, body, 0)

    def finish_ab(t):
        def own():
            AO[:, :RBS[t]] = ab_part(y, t)

        own()
        got(AR.at[:, chunk(t)], ("ab", t))

        def body(o, rs):
            ra = pl.ds(pl.multiple_of(rs.start - OFF[t], 16), 16)
            a = (AO[o, ra, :fq] + AR[o, rs, :fq]).astype(BF16).astype(F32)
            b = (AO[o, ra, fq:] + AR[o, rs, fq:]).astype(BF16).astype(F32)
            g, gd = gelu_pair(a)
            HL[hs, y, o, rs] = (g * b).astype(BF16)
            AR[o, rs, :fq] = b * gd
            AR[o, rs, fq:] = g

        row_blocks(t, body)
        send(HL.at[2, y, :, chunk(t)], HL.at[c, y, :, chunk(t)], ("hy", t), dev(r_=ro), away)

    def finish_dh(t):
        for n in NS:
            if n == NS[-1] or t == 0:
                got(DR.at[dh_cols(n, t)], ("dh", n, t))

        def body(o, rs):
            dh = DO[o, rs] + DR[o, rs]
            DB[r, o, rs, :fq] = (dh * AR[o, rs, :fq]).astype(BF16)
            DB[r, o, rs, fq:] = (dh * AR[o, rs, fq:]).astype(BF16)

        row_blocks(t, body)
        mine = DB.at[r, :, chunk(t)]
        send(mine, mine, ("dby", t), dev(r_=ro))
        send(mine, mine, ("dbd", t), dev(r_=rp))

    def relay_db(t):
        theirs = DB.at[ro, :, chunk(t)]
        got(theirs, ("dby", t))
        send(theirs, theirs, ("dbf", t), dev(r_=rp))

    def h_start(t):
        A, B = HL.at[jA, :, :, chunk(t)], HL.at[jB, :, :, chunk(t)]
        got(HL.at[c, 1 - y, :, chunk(t)], ("hy", t), home)
        send(A, A, ("hA", t), dev(z_=zf), zeta == 0, zeta <= 2)
        send(B, B, ("hB", t), dev(z_=zf), zeta == 1, both(zeta >= 1, zeta <= 2))
        send(B, B, ("hb", t), dev(z_=zb), zeta == 1)

    def h_pass(t, i):
        if i == 0:
            B = HL.at[jB, :, :, chunk(t)]
            got(B, ("hB", t), zeta == 2)
            send(B, B, ("hB", t), dev(z_=zf), zeta == 2, False)
        else:
            A = HL.at[jA, :, :, chunk(t)]
            got(A, ("hA", t), zeta == i)
            send(A, A, ("hA", t), dev(z_=zf), zeta == i, False)

    def h_last(t):
        A, B = HL.at[jA, :, :, chunk(t)], HL.at[jB, :, :, chunk(t)]
        got(B, ("hb", t), zeta == 0)
        got(B, ("hB", t), zeta == 3)
        got(A, ("hA", t), zeta == 3)
        send(HL.at[1 - k, :, :, chunk(t)], HP.at[:, :, chunk(t)], ("hd", t), dev(r_=rp))
        out(HL.at[k, :, :, chunk(t)], ho.at[:, k, :, chunk(t)], "ho", t)

    outs = []

    def out(src, dst, *name):
        cp = local(src, dst, *name)
        cp.start()
        outs.append(cp)

    target = jnp.where(y == 0, k, 1 - k)
    top = NCH - 1

    def dx_part(t, i):
        q = (r, rp, ro, rx)[i]
        theirs = DB.at[q, :, chunk(t)]
        if i == 1:
            got(theirs, ("dbd", t))
        if i == 3:
            got(theirs, ("dbf", t))
            out(DB.at[:, :, chunk(t)], dbo.at[:, :, chunk(t)], "dbo", t)
        sl = slice(OFF[t], OFF[t] + RBS[t])

        def go():
            d = lax.dot_general(DB[q, :, sl].reshape(4 * RBS[t], 2 * fq), WV[q], NT_DIMS, preferred_element_type=F32).reshape(2, 2, RBS[t], cm)
            DXS[:, :, sl] = d if i == 0 else DXS[:, :, sl] + d

        go()
        if i < 3:
            return
        mine = DXS.at[:, :, chunk(t)]
        if t < top:
            send(mine, DXA.at[:, :, chunk(t)], ("dxa", t), dev(z_=zb), zeta == 3, False)
            send(mine, DXM.at[:, :, chunk(t)], ("dxm", t), dev(z_=zf), both(zeta == 0, target == 1))
        else:
            send(DXS.at[1 - c, :, chunk(t)], DXA.at[0, :, chunk(t)], ("dx1",), dev(z_=zm))

    def dx_add(t, cond, parts):
        sl = slice(OFF[t], OFF[t] + RBS[t])

        def go():
            for ref in parts:
                DXS[:, :, sl] += ref[:, :, sl]

        pl.when(cond)(go)

    def dx_step(t, at):
        on = zeta == at
        goes = both(on, at > target) if at else both(on, target < 0)
        got(DXA.at[:, :, chunk(t)], ("dxa", t), both(on, at >= target))
        if at == 1:
            got(DXM.at[:, :, chunk(t)], ("dxm", t), both(on, target == 1))
            dx_add(t, both(on, target == 1), (DXA, DXM))
            dx_add(t, both(on, target == 0), (DXA,))
        else:
            dx_add(t, both(on, at >= target), (DXA,))
        if at:
            send(DXS.at[:, :, chunk(t)], DXA.at[:, :, chunk(t)], ("dxa", t), dev(z_=zb), goes, both(zeta >= 1, zeta > target) if at == 1 else False)

    def dx_spread(t):
        sl = slice(OFF[t], OFF[t] + RBS[t])

        @pl.when(diag)
        def _():
            DXF.__setitem__((slice(None), slice(None), sl), DXS[:, :, sl].astype(BF16))

        for k2, y2, i in ((1 - k, y, 0), (k, 1 - y, 1), (1 - k, 1 - y, 2)):
            send(DXF.at[k2, y2, chunk(t)], DXR.at[chunk(t)], ("dxf", t, i), dev(r_=2 * y2 + k2), diag)

    def dx_half():
        t = top
        sl = slice(OFF[t], OFF[t] + RBS[t])
        got(DXA.at[0, :, chunk(t)], ("dx1",))

        def go():
            DXS[c, :, sl] += DXA[0, :, sl]

        go()
        send(DXS.at[c, 1 - pr, chunk(t)], DXM.at[0, 0, chunk(t)], ("dx2",), dev(z_=zt))

    def dx_quarter():
        t = top
        sl = slice(OFF[t], OFF[t] + RBS[t])
        got(DXM.at[0, 0, chunk(t)], ("dx2",))

        def go():
            DXF[k, y, sl] = (DXS[c, pr, sl] + DXM[0, 0, sl]).astype(BF16)

        go()
        send(DXF.at[k, y, chunk(t)], DXR.at[chunk(t)], ("dxt",), dev(z_=r, r_=z), jnp.logical_not(diag))

    def start():
        send(gy_hbm, DY.at[c, k, y], ("dyy",), dev(r_=ro))
        x_send(0)
        for m, w in enumerate((wg_hbm, wu_hbm)):
            for s in range(2):
                send(w.at[:, pl.ds(pl.multiple_of((1 - k + 2 * s) * fq, 128), fq)], WP.at[s, :, pl.ds(m * fq, fq)], ("w", m, s), dev(r_=rp))
        wo_far(0, away)
        wo_near(0, home)
        wo_near(0, away)

    def h_take(t):
        got(HP.at[:, :, chunk(t)], ("hd", t))
        out(HP.at[:, :, chunk(t)], ho.at[:, 1 - k, :, chunk(t)], "hp", t)

    def dx_take(t):
        sl = slice(OFF[t], OFF[t] + RBS[t])
        zk, zy = z % 2, z // 2

        @pl.when(diag)
        def _():
            DXR.__setitem__(sl, DXF[k, y, sl])

        if t < top:
            got(DXR.at[chunk(t)], ("dxf", t, 0), both(zk != k, zy == y))
            got(DXR.at[chunk(t)], ("dxf", t, 1), both(zk == k, zy != y))
            got(DXR.at[chunk(t)], ("dxf", t, 2), both(zk != k, zy != y))
        else:
            got(DXR.at[chunk(t)], ("dxt",), jnp.logical_not(diag))

    def out_early():
        XT.__setitem__(Ellipsis, XG[k].reshape(4 * rows, cm).T)
        out(XT, xo, "xo")
        out(DY.at[c], dyo, "dyo")

    start()
    wo_near(2, home)
    x_step(0, 1, 0)
    x_step(0, 1, 1)
    wo_far(0, home)
    x_send(1)
    x_step(0, 2, 0)
    x_step(0, 2, 1)
    wo_far(2, home)
    wo_pass(1, 0, home)
    weights_here()
    wo_near(2, away)
    wo_near(1, home)
    wo_relay(0, home)
    x_step(1, 1, 0)
    wo_far(1, away)
    wo_near(1, away)
    x_step(0, 3, 0)
    x_step(0, 3, 1)
    wo_relay(0, away)
    x_give(0)
    wo_pass(1, 0, away)
    x_step(1, 1, 1)
    x_take(0)
    dy_pass()
    x_step(1, 2, 0)
    wo_pass(1, 1, away)
    wo_pass(2, 1, away)
    ab_mirror(0, home, True)
    wo_relay(1, away)
    wo_pass(2, 0, away)
    wo_pass(3, 0, home)
    x_step(1, 2, 1)
    wo_pass(1, 1, home)
    ab_mirror(0, away, False)
    wo_far(1, home)
    dy_give()
    wo_pass(2, 0, home)
    wo_pass(3, 0, away)
    wo_pass(1, 2, home)
    wo_far(2, away)
    wo_relay(2, home)
    wo_pass(1, 2, away)
    wo_pass(3, 1, home)
    dy_take()
    dh_mirror(0)
    dh_mirror(1)
    finish_ab(0)
    x_step(1, 3, 1)
    wo_pass(2, 2, away)
    wo_relay(2, away)
    wo_pass(2, 1, home)
    ab_mirror(1)
    x_step(1, 3, 0)
    x_give(1)
    wo_pass(3, 2, away)
    wo_relay(1, home)
    dh_own(0)
    wo_pass(3, 2, home)
    wo_pass(2, 2, home)
    dh_mirror(2)
    x_take(1)
    ab_mirror(3)
    wo_pass(3, 1, away)
    h_start(0)
    dh_own(2)
    dh_own(1)
    finish_dh(0)
    out_early()
    finish_ab(1)
    ab_mirror(2)
    dx_part(0, 0)
    h_pass(0, 1)
    finish_ab(3)
    relay_db(0)
    finish_dh(1)
    dx_part(0, 1)
    h_pass(0, 0)
    dx_part(0, 2)
    dx_part(0, 3)
    h_start(1)
    finish_ab(2)
    finish_dh(3)
    h_pass(1, 1)
    h_start(3)
    h_pass(0, 2)
    finish_dh(2)
    dx_part(1, 0)
    dx_step(0, 2)
    dx_part(1, 1)
    h_pass(3, 1)
    relay_db(1)
    h_pass(1, 0)
    h_start(2)
    dx_part(1, 2)
    dx_part(1, 3)
    dx_step(0, 1)
    h_pass(1, 2)
    h_last(0)
    relay_db(3)
    dx_part(2, 0)
    relay_db(2)
    dx_part(2, 1)
    dx_part(2, 2)
    dx_step(1, 2)
    dx_part(3, 0)
    dx_part(3, 1)
    h_pass(2, 1)
    dx_part(2, 3)
    dx_part(3, 2)
    h_pass(3, 2)
    dx_part(3, 3)
    h_last(1)
    dx_step(0, 0)
    dx_step(2, 2)
    h_take(0)
    dx_step(1, 1)
    h_pass(2, 0)
    h_pass(3, 0)
    h_take(1)
    h_last(3)
    dx_step(1, 0)
    h_take(3)
    dx_spread(1)
    dx_spread(0)
    dx_half()
    dx_step(2, 1)
    dx_step(2, 0)
    dx_spread(2)
    dx_quarter()
    h_pass(2, 2)
    dx_take(0)
    h_last(2)
    dx_take(1)
    dx_take(3)
    dx_take(2)
    h_take(2)

    out(DXR, dxo, "dxo")
    for cond, cp in pending:
        if cond is None:
            cp.wait_send()
        else:
            pl.when(cond)(cp.wait_send)
    for cp in outs:
        cp.wait()


def dw_kernel(x_hbm, dy_hbm, db_hbm, h_hbm, dx_hbm, dwg, dwu, dwo, dxo, XT, DY, DB, H, OA, OB, in_sem, out_sem):
    fq = H.shape[-1]
    loads = [pltpu.make_async_copy(x_hbm, XT, in_sem.at[0])]
    loads += [pltpu.make_async_copy(db_hbm.at[q], DB.at[q], in_sem.at[1 + q]) for q in range(4)]
    loads += [pltpu.make_async_copy(dy_hbm, DY, in_sem.at[5])]
    loads += [pltpu.make_async_copy(h_hbm.at[q], H.at[q], in_sem.at[6 + q]) for q in range(4)]
    for cp in loads:
        cp.start()
    outs = []

    def put(src, dst):
        cp = pltpu.make_async_copy(src, dst, out_sem.at[len(outs)])
        cp.start()
        outs.append(cp)

    loads[0].wait()
    for q in range(4):
        loads[1 + q].wait()
        OA[q] = jnp.dot(XT[...], DB[q], preferred_element_type=F32)
        for m, dst in enumerate((dwg, dwu)):
            put(OA.at[q, :, pl.ds(m * fq, fq)], dst.at[:, pl.ds(q * fq, fq)])
    loads[5].wait()
    for q in range(4):
        loads[6 + q].wait()
        OB[q] = lax.dot_general(H[q], DY[...], TN_DIMS, preferred_element_type=F32)
        put(OB.at[q], dwo.at[pl.ds(q * fq, fq)])
    dxo[...] = dx_hbm[...]
    for cp in outs:
        cp.wait()


def solution(mesh):
    act_spec = P(("dp", "row"), "col")
    weight_spec = P("row", "col")

    def block_backward(x_blk, gy_blk, gate_blk, up_blk, out_blk):
        rows, dm = x_blk.shape
        ff = gate_blk.shape[1]
        fq, tok = ff // 4, 4 * rows
        vm = pltpu.VMEM
        xg, dyg, dbg, hg, dxg = pl.pallas_call(
            lambda *refs: comm_kernel(rows, dm, ff, *refs),
            out_shape=[
                jax.ShapeDtypeStruct((dm, tok), BF16),
                jax.ShapeDtypeStruct((2, 2, rows, dm), BF16),
                jax.ShapeDtypeStruct((4, 4, rows, 2 * fq), BF16),
                jax.ShapeDtypeStruct((2, 2, 4, rows, fq), BF16),
                jax.ShapeDtypeStruct((rows, dm), BF16),
            ],
            in_specs=[ANY] * 5,
            out_specs=[ANY] * 5,
            scratch_shapes=[
                vm((2, 2, 2, rows, dm), BF16),
                vm((2, rows, dm), BF16),
                vm((2, 2, 2, rows, dm), BF16),
                vm((4, dm, 2 * fq), BF16),
                vm((2, dm, 2 * fq), BF16),
                vm((2, fq, 2 * dm), BF16),
                vm((fq, dm // 2), BF16),
                vm((4, rows, 2 * fq), F32),
                vm((4, rows, 2 * fq), F32),
                vm((4, max(RBS), 2 * fq), F32),
                vm((4, rows, fq), F32),
                vm((4, rows, fq), F32),
                vm((4, rows, fq), F32),
                vm((4, 4, rows, 2 * fq), BF16),
                vm((3, 2, 4, rows, fq), BF16),
                vm((2, 4, rows, fq), BF16),
                vm((2, 2, rows, dm), F32),
                vm((2, 2, rows, dm), F32),
                vm((2, 2, rows, dm), F32),
                vm((2, 2, rows, dm), BF16),
                vm((rows, dm), BF16),
                vm((dm, tok), BF16),
                pltpu.SemaphoreType.DMA((N_SEND,)),
                pltpu.SemaphoreType.DMA((N_RECV,)),
                pltpu.SemaphoreType.DMA((N_LOCAL,)),
            ],
            compiler_params=pltpu.CompilerParams(collective_id=0, has_side_effects=True, vmem_limit_bytes=63 * 1024 * 1024),
            name="comm",
        )(x_blk, gy_blk, gate_blk, up_blk, out_blk)
        whole = pl.BlockSpec(memory_space=vm)
        dw_gate, dw_up, dw_out, grad_x = pl.pallas_call(
            dw_kernel,
            out_shape=[
                jax.ShapeDtypeStruct((dm, ff), F32),
                jax.ShapeDtypeStruct((dm, ff), F32),
                jax.ShapeDtypeStruct((ff, dm), F32),
                jax.ShapeDtypeStruct((rows, dm), BF16),
            ],
            in_specs=[ANY] * 4 + [whole],
            out_specs=[ANY] * 3 + [whole],
            scratch_shapes=[
                vm((dm, tok), BF16), vm((tok, dm), BF16),
                vm((4, tok, 2 * fq), BF16), vm((4, tok, fq), BF16),
                vm((4, dm, 2 * fq), F32), vm((4, fq, dm), F32),
                pltpu.SemaphoreType.DMA((10,)), pltpu.SemaphoreType.DMA((12,)),
            ],
            compiler_params=pltpu.CompilerParams(vmem_limit_bytes=60 * 1024 * 1024),
            name="dw",
        )(xg, dyg.reshape(tok, dm), dbg.reshape(4, tok, 2 * fq), hg.reshape(4, tok, fq), dxg)
        return grad_x, dw_gate, dw_up, dw_out

    return jax.shard_map(block_backward, mesh=mesh, in_specs=(act_spec, act_spec, weight_spec, weight_spec, weight_spec), out_specs=(act_spec, act_spec, act_spec, act_spec), check_vma=False)
```

time: 1510 us -> 218 us (0.14)
  waiting for transfers between devices: 1360 us -> 0 us
  Pallas kernels: 0 us -> 217 us
  matrix products: 111 us -> 0 us
  local copies, waits for them, and re-layouts: 22.8 us -> 0 us
    reduce_scatter x5 -> x0, waiting for transfers between devices: 950 us -> none  [the longest x1 281 us: block_backward(): lax.psum_scatter(lax.dot_general(x_band, grad_gate, COL_DIMS, preferred_e...]
    all_gather x5 -> x0, waiting for transfers between devices: 407 us -> none  [the longest x1 135 us: block_backward(): out_band = lax.all_gather(out_blk, 'row', axis=0, tiled=True)]
    pallas_call x0 -> x2, Pallas kernels: none -> 217 us  [the longest x1 201 us: block_backward(): pl.pallas_call(lambda *refs: comm_kernel(rows, dm, ff, *refs), out_shape=...]
    dot_general x8 -> x0, matrix products: 111 us -> none  [the longest x1 18.1 us: block_backward(): lax.dot_general(hidden_band, gy_blk, COL_DIMS, preferred_element_type=jnp...]
    unnamed x6 -> x0, local copies, waits for them, and re-layouts: 22.8 us -> none
  transfers between devices with their start and end apart: 10 -> 0, of which waited for: 9 -> 0; matrix products, arithmetic and copies ran while one was open for 8% -> 0% of each run, Pallas kernels for 0% -> 0%
where the time goes in v3:
time: 218 us
  Pallas kernels  217 us (100%)
    pallas_call x1, Pallas kernels, block_backward(): pl.pallas_call(lambda *refs: comm_kernel(rows, dm, ff, *refs), out_shape=...  201 us
    pallas_call x1, Pallas kernels, block_backward(): pl.pallas_call(dw_kernel, out_shape=[jax.ShapeDtypeStruct((dm, ff), F32),...  16.1 us

profile of v3, /device:TPU:0, one launch (start us, length us, event | category | flops | bytes accessed | tf_op | source)
XLA Modules:
  0.0 217.7 jit_solution(5061914597666666937)
XLA Ops:
  0.6 200.8 %comm.1 = (bf16[1024,512]{1,0:T(8,128)(2,1)}, bf16[2,2,128,1024]{3,2,1,0:T(8,128)(2,1)}, bf16[4,4,128,1280]{3,2,1,0:T(8,128)(2,1)}, bf16[2,2,4,128,640]{4,3,2,1,0:T(8,128)(2,1)}, bf16[128,1024]{1,0:T(8,128)(2,1)}) custom-call(bf16[128,1024]{1,0:T(8,128)(2,1)} %refs_0_.1, bf16[128,1024]{1,0:T(8,128)(2,1)} %refs_1_.1, bf16[1024,2560]{1,0:T(8,128)(2,1)} %refs_2_.1, ...), custom_call_target="tpu_custom_call" | custom-call | tf_op jit(solution)/shard_map/comm/pallas_call | solution.py:657
  201.4 16.1 %dw.1 = (f32[1024,2560]{1,0:T(8,128)}, f32[1024,2560]{1,0:T(8,128)}, f32[2560,1024]{1,0:T(8,128)}, bf16[128,1024]{1,0:T(8,128)(2,1)}) custom-call(bf16[1024,512]{1,0:T(8,128)(2,1)} %get-tuple-element.13.x_hbm, bf16[512,1024]{1,0:T(8,128)(2,1)} %bitcast.5, bf16[4,512,1280]{2,1,0:T(8,128)(2,1)} %bitcast.3, bf16[4,512,640]{2,1,0:T(8,128)(2,1)} %bitcast.4, ...), custom_call_target="tpu_custom_call" | custom-call | tf_op jit(solution)/shard_map/dw/pallas_call | solution.py:699

commit v4 on v3

--- a/solution.py
+++ b/solution.py
@@ -12,13 +12,14 @@
 ANY = pl.BlockSpec(memory_space=pl.ANY)
 NT_DIMS = (((1,), (1,)), ((), ()))
 TN_DIMS = (((0,), (0,)), ((), ()))
-RBS = (48, 32, 32, 16)
+RBS = (32, 32, 32, 32)
 NCH = len(RBS)
+CHAIN = 3
 OFF = tuple(sum(RBS[:t]) for t in range(NCH))
-X_CUT = ((0, 80), (80, 48))
+X_CUT = ((0, 64), (64, 64))
 N_CUT = ((0, 128), (128, 256), (384, 256))
 NS = range(len(N_CUT))
-N_SEND, N_RECV, N_LOCAL = 160, 160, 48
+N_SEND, N_RECV, N_LOCAL = 240, 240, 64
 
 
 def gelu_pair(pre_f32):
@@ -190,13 +191,12 @@
             q = 2 * (1 - y) + k2
             send(wo_cut(q, n, pcols), wo_slot(role, n, c, (p * half, half)), ("wo", 1, n, k2), dev(r_=q), both(cond, k == c))
 
-    def wo_far(n, cond):
+    def wo_far(n, over, cond):
         off, ln = N_CUT[n]
-        for over in (0, 1):
-            for k2 in range(2):
-                q = 2 * (1 - y if over else y) + k2
-                dst = WR.at[pl.ds(off, ln)] if over else wo_slot(role, n, c, (p * half, half))
-                send(wo_cut(q, n, pcols), dst, ("wf" if over else "wo", 2, n, k2), dev(z_=zm, r_=2 * y + k2), both(cond, k != c))
+        for k2 in range(2):
+            q = 2 * (1 - y if over else y) + k2
+            dst = WR.at[pl.ds(off, ln)] if over else wo_slot(role, n, c, (p * half, half))
+            send(wo_cut(q, n, pcols), dst, ("wf" if over else "wo", 2, n, k2), dev(z_=zm, r_=2 * y + k2), both(cond, k != c))
 
     def wo_relay(n, cond):
         off, ln = N_CUT[n]
@@ -352,7 +352,10 @@
         outs.append(cp)
 
     target = jnp.where(y == 0, k, 1 - k)
-    top = NCH - 1
+
+    def piece(u):
+        t, ln = u // 2, RBS[u // 2] // 2
+        return OFF[t] + u % 2 * ln, ln
 
     def dx_part(t, i):
         q = (r, rp, ro, rx)[i]
@@ -371,15 +374,17 @@
         go()
         if i < 3:
             return
-        mine = DXS.at[:, :, chunk(t)]
-        if t < top:
-            send(mine, DXA.at[:, :, chunk(t)], ("dxa", t), dev(z_=zb), zeta == 3, False)
-            send(mine, DXM.at[:, :, chunk(t)], ("dxm", t), dev(z_=zf), both(zeta == 0, target == 1))
-        else:
-            send(DXS.at[1 - c, :, chunk(t)], DXA.at[0, :, chunk(t)], ("dx1",), dev(z_=zm))
-
-    def dx_add(t, cond, parts):
-        sl = slice(OFF[t], OFF[t] + RBS[t])
+        if t < CHAIN:
+            for u in (2 * t, 2 * t + 1):
+                rs = pl.ds(*piece(u))
+                send(DXS.at[:, :, rs], DXA.at[:, :, rs], ("dxa", u), dev(z_=zb), zeta == 3, False)
+                send(DXS.at[:, :, rs], DXM.at[:, :, rs], ("dxm", u), dev(z_=zf), both(zeta == 0, target == 1))
+        else:
+            send(DXS.at[1 - c, :, chunk(t)], DXA.at[0, :, chunk(t)], ("dx1", t), dev(z_=zm))
+
+    def dx_add(u, cond, parts):
+        off, ln = piece(u)
+        sl = slice(off, off + ln)
 
         def go():
             for ref in parts:
@@ -387,60 +392,58 @@
 
         pl.when(cond)(go)
 
-    def dx_step(t, at):
+    def dx_step(u, at):
+        rs = pl.ds(*piece(u))
         on = zeta == at
         goes = both(on, at > target) if at else both(on, target < 0)
-        got(DXA.at[:, :, chunk(t)], ("dxa", t), both(on, at >= target))
+        got(DXA.at[:, :, rs], ("dxa", u), both(on, at >= target))
         if at == 1:
-            got(DXM.at[:, :, chunk(t)], ("dxm", t), both(on, target == 1))
-            dx_add(t, both(on, target == 1), (DXA, DXM))
-            dx_add(t, both(on, target == 0), (DXA,))
-        else:
-            dx_add(t, both(on, at >= target), (DXA,))
+            got(DXM.at[:, :, rs], ("dxm", u), both(on, target == 1))
+            dx_add(u, both(on, target == 1), (DXA, DXM))
+            dx_add(u, both(on, target == 0), (DXA,))
+        else:
+            dx_add(u, both(on, at >= target), (DXA,))
         if at:
-            send(DXS.at[:, :, chunk(t)], DXA.at[:, :, chunk(t)], ("dxa", t), dev(z_=zb), goes, both(zeta >= 1, zeta > target) if at == 1 else False)
-
-    def dx_spread(t):
-        sl = slice(OFF[t], OFF[t] + RBS[t])
+            send(DXS.at[:, :, rs], DXA.at[:, :, rs], ("dxa", u), dev(z_=zb), goes, both(zeta >= 1, zeta > target) if at == 1 else False)
+
+    def dx_spread(u):
+        off, ln = piece(u)
+        sl, rs = slice(off, off + ln), pl.ds(off, ln)
 
         @pl.when(diag)
         def _():
             DXF.__setitem__((slice(None), slice(None), sl), DXS[:, :, sl].astype(BF16))
 
         for k2, y2, i in ((1 - k, y, 0), (k, 1 - y, 1), (1 - k, 1 - y, 2)):
-            send(DXF.at[k2, y2, chunk(t)], DXR.at[chunk(t)], ("dxf", t, i), dev(r_=2 * y2 + k2), diag)
-
-    def dx_half():
-        t = top
+            send(DXF.at[k2, y2, rs], DXR.at[rs], ("dxf", u, i), dev(r_=2 * y2 + k2), diag)
+
+    def dx_half(t):
         sl = slice(OFF[t], OFF[t] + RBS[t])
-        got(DXA.at[0, :, chunk(t)], ("dx1",))
+        got(DXA.at[0, :, chunk(t)], ("dx1", t))
 
         def go():
             DXS[c, :, sl] += DXA[0, :, sl]
 
         go()
-        send(DXS.at[c, 1 - pr, chunk(t)], DXM.at[0, 0, chunk(t)], ("dx2",), dev(z_=zt))
-
-    def dx_quarter():
-        t = top
+        send(DXS.at[c, 1 - pr, chunk(t)], DXM.at[0, 0, chunk(t)], ("dx2", t), dev(z_=zt))
+
+    def dx_quarter(t):
         sl = slice(OFF[t], OFF[t] + RBS[t])
-        got(DXM.at[0, 0, chunk(t)], ("dx2",))
+        got(DXM.at[0, 0, chunk(t)], ("dx2", t))
 
         def go():
             DXF[k, y, sl] = (DXS[c, pr, sl] + DXM[0, 0, sl]).astype(BF16)
 
         go()
-        send(DXF.at[k, y, chunk(t)], DXR.at[chunk(t)], ("dxt",), dev(z_=r, r_=z), jnp.logical_not(diag))
-
-    def start():
+        send(DXF.at[k, y, chunk(t)], DXR.at[chunk(t)], ("dxt", t), dev(z_=r, r_=z), jnp.logical_not(diag))
+
+    def dy_send():
         send(gy_hbm, DY.at[c, k, y], ("dyy",), dev(r_=ro))
-        x_send(0)
+
+    def w_swap():
         for m, w in enumerate((wg_hbm, wu_hbm)):
             for s in range(2):
                 send(w.at[:, pl.ds(pl.multiple_of((1 - k + 2 * s) * fq, 128), fq)], WP.at[s, :, pl.ds(m * fq, fq)], ("w", m, s), dev(r_=rp))
-        wo_far(0, away)
-        wo_near(0, home)
-        wo_near(0, away)
 
     def h_take(t):
         got(HP.at[:, :, chunk(t)], ("hd", t))
@@ -454,155 +457,182 @@
         def _():
             DXR.__setitem__(sl, DXF[k, y, sl])
 
-        if t < top:
-            got(DXR.at[chunk(t)], ("dxf", t, 0), both(zk != k, zy == y))
-            got(DXR.at[chunk(t)], ("dxf", t, 1), both(zk == k, zy != y))
-            got(DXR.at[chunk(t)], ("dxf", t, 2), both(zk != k, zy != y))
-        else:
-            got(DXR.at[chunk(t)], ("dxt",), jnp.logical_not(diag))
+        if t < CHAIN:
+            for u in (2 * t, 2 * t + 1):
+                rs = pl.ds(*piece(u))
+                got(DXR.at[rs], ("dxf", u, 0), both(zk != k, zy == y))
+                got(DXR.at[rs], ("dxf", u, 1), both(zk == k, zy != y))
+                got(DXR.at[rs], ("dxf", u, 2), both(zk != k, zy != y))
+        else:
+            got(DXR.at[chunk(t)], ("dxt", t), jnp.logical_not(diag))
 
     def out_early():
         XT.__setitem__(Ellipsis, XG[k].reshape(4 * rows, cm).T)
         out(XT, xo, "xo")
         out(DY.at[c], dyo, "dyo")
 
-    start()
-    wo_near(2, home)
-    x_step(0, 1, 0)
-    x_step(0, 1, 1)
-    wo_far(0, home)
-    x_send(1)
-    x_step(0, 2, 0)
-    x_step(0, 2, 1)
-    wo_far(2, home)
-    wo_pass(1, 0, home)
+    i0, i1, i2, i3, i4, i5, i6, i7, i8, i9 = range(10)
+    yes, no = True, False
+    wo_near(i1, home)
+    wo_far(i0, i1, home)
+    x_send(i0)
+    wo_near(i2, home)
+    wo_far(i1, i0, home)
+    dy_send()
+    wo_far(i2, i1, home)
+    wo_far(i0, i1, away)
+    wo_relay(i0, home)
+    x_send(i1)
+    wo_near(i0, away)
+    wo_far(i1, i1, away)
+    w_swap()
+    wo_pass(i2, i1, home)
+    x_step(i0, i1, i1)
+    wo_relay(i2, home)
+    x_step(i0, i1, i0)
+    x_step(i1, i1, i1)
+    x_step(i1, i1, i0)
+    wo_near(i1, away)
+    wo_pass(i3, i0, away)
+    wo_far(i0, i0, away)
+    x_step(i0, i2, i1)
     weights_here()
-    wo_near(2, away)
-    wo_near(1, home)
-    wo_relay(0, home)
-    x_step(1, 1, 0)
-    wo_far(1, away)
-    wo_near(1, away)
-    x_step(0, 3, 0)
-    x_step(0, 3, 1)
-    wo_relay(0, away)
-    x_give(0)
-    wo_pass(1, 0, away)
-    x_step(1, 1, 1)
-    x_take(0)
+    wo_far(i0, i0, home)
+    x_step(i0, i2, i0)
+    wo_relay(i0, away)
+    x_step(i1, i2, i0)
+    x_step(i1, i2, i1)
     dy_pass()
-    x_step(1, 2, 0)
-    wo_pass(1, 1, away)
-    wo_pass(2, 1, away)
-    ab_mirror(0, home, True)
-    wo_relay(1, away)
-    wo_pass(2, 0, away)
-    wo_pass(3, 0, home)
-    x_step(1, 2, 1)
-    wo_pass(1, 1, home)
-    ab_mirror(0, away, False)
-    wo_far(1, home)
+    wo_far(i2, i0, home)
+    x_step(i0, i3, i0)
+    wo_far(i1, i1, home)
+    wo_pass(i1, i0, home)
+    wo_far(i1, i0, away)
+    wo_near(i0, home)
+    wo_near(i2, away)
+    x_step(i1, i3, i0)
+    wo_pass(i1, i1, home)
+    wo_pass(i3, i0, home)
+    wo_pass(i2, i0, home)
+    wo_pass(i1, i2, away)
+    wo_relay(i1, away)
+    x_step(i0, i3, i1)
+    x_give(i0)
+    x_take(i0)
+    x_step(i1, i3, i1)
+    wo_pass(i1, i1, away)
+    ab_mirror(i1)
+    x_give(i1)
+    x_take(i1)
+    ab_mirror(i2)
+    ab_mirror(i0, home, yes)
+    wo_pass(i1, i0, away)
+    wo_far(i2, i0, away)
+    wo_pass(i2, i0, away)
     dy_give()
-    wo_pass(2, 0, home)
-    wo_pass(3, 0, away)
-    wo_pass(1, 2, home)
-    wo_far(2, away)
-    wo_relay(2, home)
-    wo_pass(1, 2, away)
-    wo_pass(3, 1, home)
+    wo_pass(i3, i1, home)
+    wo_far(i2, i1, away)
     dy_take()
-    dh_mirror(0)
-    dh_mirror(1)
-    finish_ab(0)
-    x_step(1, 3, 1)
-    wo_pass(2, 2, away)
-    wo_relay(2, away)
-    wo_pass(2, 1, home)
-    ab_mirror(1)
-    x_step(1, 3, 0)
-    x_give(1)
-    wo_pass(3, 2, away)
-    wo_relay(1, home)
-    dh_own(0)
-    wo_pass(3, 2, home)
-    wo_pass(2, 2, home)
-    dh_mirror(2)
-    x_take(1)
-    ab_mirror(3)
-    wo_pass(3, 1, away)
-    h_start(0)
-    dh_own(2)
-    dh_own(1)
-    finish_dh(0)
+    dh_mirror(i0)
+    wo_pass(i1, i2, home)
+    wo_pass(i2, i1, away)
+    dh_mirror(i1)
+    wo_relay(i1, home)
+    wo_relay(i2, away)
+    wo_pass(i2, i2, away)
+    finish_ab(i2)
+    wo_pass(i3, i2, home)
+    h_start(i2)
+    dh_own(i0)
+    wo_pass(i3, i2, away)
+    dh_mirror(i2)
+    ab_mirror(i0, away, no)
+    finish_ab(i1)
+    wo_pass(i2, i2, home)
+    ab_mirror(i3)
     out_early()
-    finish_ab(1)
-    ab_mirror(2)
-    dx_part(0, 0)
-    h_pass(0, 1)
-    finish_ab(3)
-    relay_db(0)
-    finish_dh(1)
-    dx_part(0, 1)
-    h_pass(0, 0)
-    dx_part(0, 2)
-    dx_part(0, 3)
-    h_start(1)
-    finish_ab(2)
-    finish_dh(3)
-    h_pass(1, 1)
-    h_start(3)
-    h_pass(0, 2)
-    finish_dh(2)
-    dx_part(1, 0)
-    dx_step(0, 2)
-    dx_part(1, 1)
-    h_pass(3, 1)
-    relay_db(1)
-    h_pass(1, 0)
-    h_start(2)
-    dx_part(1, 2)
-    dx_part(1, 3)
-    dx_step(0, 1)
-    h_pass(1, 2)
-    h_last(0)
-    relay_db(3)
-    dx_part(2, 0)
-    relay_db(2)
-    dx_part(2, 1)
-    dx_part(2, 2)
-    dx_step(1, 2)
-    dx_part(3, 0)
-    dx_part(3, 1)
-    h_pass(2, 1)
-    dx_part(2, 3)
-    dx_part(3, 2)
-    h_pass(3, 2)
-    dx_part(3, 3)
-    h_last(1)
-    dx_step(0, 0)
-    dx_step(2, 2)
-    h_take(0)
-    dx_step(1, 1)
-    h_pass(2, 0)
-    h_pass(3, 0)
-    h_take(1)
-    h_last(3)
-    dx_step(1, 0)
-    h_take(3)
-    dx_spread(1)
-    dx_spread(0)
-    dx_half()
-    dx_step(2, 1)
-    dx_step(2, 0)
-    dx_spread(2)
-    dx_quarter()
-    h_pass(2, 2)
-    dx_take(0)
-    h_last(2)
-    dx_take(1)
-    dx_take(3)
-    dx_take(2)
-    h_take(2)
+    dh_own(i2)
+    wo_pass(i3, i1, away)
+    finish_ab(i0)
+    dh_own(i1)
+    finish_dh(i0)
+    finish_dh(i1)
+    h_start(i1)
+    finish_ab(i3)
+    dx_part(i1, i0)
+    dx_part(i0, i0)
+    h_start(i0)
+    h_pass(i2, i0)
+    finish_dh(i2)
+    relay_db(i0)
+    dx_part(i0, i1)
+    finish_dh(i3)
+    h_pass(i2, i1)
+    dx_part(i0, i2)
+    dx_part(i0, i3)
+    dx_part(i1, i1)
+    relay_db(i1)
+    h_pass(i1, i0)
+    h_start(i3)
+    dx_part(i1, i2)
+    dx_part(i1, i3)
+    dx_part(i2, i0)
+    h_pass(i0, i1)
+    dx_step(i0, i2)
+    h_pass(i0, i0)
+    dx_part(i2, i1)
+    relay_db(i2)
+    h_pass(i1, i1)
+    dx_part(i2, i2)
+    dx_part(i3, i0)
+    dx_step(i1, i2)
+    dx_step(i0, i1)
+    dx_part(i2, i3)
+    dx_step(i1, i1)
+    relay_db(i3)
+    dx_step(i0, i0)
+    h_pass(i2, i2)
+    dx_part(i3, i1)
+    dx_step(i2, i2)
+    dx_step(i2, i1)
+    dx_part(i3, i2)
+    dx_part(i3, i3)
+    dx_step(i2, i0)
+    h_pass(i3, i0)
+    dx_spread(i2)
+    dx_step(i3, i2)
+    dx_step(i3, i1)
+    dx_step(i1, i0)
+    h_pass(i0, i2)
+    h_pass(i3, i1)
+    dx_step(i4, i2)
+    dx_step(i5, i2)
+    dx_step(i3, i0)
+    dx_step(i4, i1)
+    dx_spread(i1)
+    dx_half(i3)
+    dx_step(i4, i0)
+    h_last(i2)
+    dx_spread(i0)
+    dx_spread(i3)
+    dx_spread(i4)
+    dx_step(i5, i1)
+    dx_step(i5, i0)
+    h_last(i0)
+    dx_spread(i5)
+    h_pass(i1, i2)
+    dx_quarter(i3)
+    h_pass(i3, i2)
+    h_last(i1)
+    dx_take(i1)
+    dx_take(i2)
+    h_take(i0)
+    h_take(i1)
+    h_take(i2)
+    dx_take(i3)
+    h_last(i3)
+    dx_take(i0)
+    h_take(i3)
 
     out(DXR, dxo, "dxo")
     for cond, cp in pending:

time: 218 us -> 203 us (0.931)
  Pallas kernels: 217 us -> 200 us
    pallas_call x1, Pallas kernels: 201 us -> 184 us  [block_backward(): pl.pallas_call(lambda *refs: comm_kernel(rows, dm, ff, *refs), out_shape=...]
where the time goes in v4:
time: 203 us; the launch traced here: 201 us
  Pallas kernels  200 us (99%)
    pallas_call x1, Pallas kernels, block_backward(): pl.pallas_call(lambda *refs: comm_kernel(rows, dm, ff, *refs), out_shape=...  184 us
    pallas_call x1, Pallas kernels, block_backward(): pl.pallas_call(dw_kernel, out_shape=[jax.ShapeDtypeStruct((dm, ff), F32),...  16.1 us

profile of v4, /device:TPU:0, one launch (start us, length us, event | category | flops | bytes accessed | tf_op | source)
XLA Modules:
  0.0 201.1 jit_solution(6704057260658747006)
XLA Ops:
  0.6 184.3 %comm.1 = (bf16[1024,512]{1,0:T(8,128)(2,1)}, bf16[2,2,128,1024]{3,2,1,0:T(8,128)(2,1)}, bf16[4,4,128,1280]{3,2,1,0:T(8,128)(2,1)}, bf16[2,2,4,128,640]{4,3,2,1,0:T(8,128)(2,1)}, bf16[128,1024]{1,0:T(8,128)(2,1)}) custom-call(bf16[128,1024]{1,0:T(8,128)(2,1)} %refs_0_.1, bf16[128,1024]{1,0:T(8,128)(2,1)} %refs_1_.1, bf16[1024,2560]{1,0:T(8,128)(2,1)} %refs_2_.1, ...), custom_call_target="tpu_custom_call" | custom-call | tf_op jit(solution)/shard_map/comm/pallas_call | solution.py:687
  184.9 16.1 %dw.1 = (f32[1024,2560]{1,0:T(8,128)}, f32[1024,2560]{1,0:T(8,128)}, f32[2560,1024]{1,0:T(8,128)}, bf16[128,1024]{1,0:T(8,128)(2,1)}) custom-call(bf16[1024,512]{1,0:T(8,128)(2,1)} %get-tuple-element.13.x_hbm, bf16[512,1024]{1,0:T(8,128)(2,1)} %bitcast.5, bf16[4,512,1280]{2,1,0:T(8,128)(2,1)} %bitcast.3, bf16[4,512,640]{2,1,0:T(8,128)(2,1)} %bitcast.4, ...), custom_call_target="tpu_custom_call" | custom-call | tf_op jit(solution)/shard_map/dw/pallas_call | solution.py:729

commit v5 on v4

--- a/solution.py
+++ b/solution.py
@@ -16,8 +16,9 @@
 NCH = len(RBS)
 CHAIN = 3
 OFF = tuple(sum(RBS[:t]) for t in range(NCH))
+PIECES = tuple((t, OFF[t] + h * n, n) for t in range(CHAIN) for n in (RBS[t] // (2 if RBS[t] % 32 == 0 else 1),) for h in range(RBS[t] // n))
 X_CUT = ((0, 64), (64, 64))
-N_CUT = ((0, 128), (128, 256), (384, 256))
+N_CUT = ((0, 256), (256, 384))
 NS = range(len(N_CUT))
 N_SEND, N_RECV, N_LOCAL = 240, 240, 64
 
@@ -32,18 +33,21 @@
 
 class Slots:
     def __init__(self, ref, size):
-        self.ref, self.size, self.names = ref, size, {}
-
-    def __call__(self, *name):
-        i = self.names.setdefault(name, len(self.names))
-        assert i < self.size
-        return self.ref.at[i]
+        self.ref, self.size, self.names, self.used = ref, size, {}, 0
+
+    def __call__(self, *name, off=None):
+        if name not in self.names:
+            self.names[name] = self.used
+            self.used += 1 if off is None else 4
+            assert self.used <= self.size
+        i = self.names[name]
+        return self.ref.at[i if off is None else i + off]
 
 
 def comm_kernel(rows, dm, ff,
                 x_hbm, gy_hbm, wg_hbm, wu_hbm, wo_hbm,
                 xo, dyo, dbo, ho, dxo,
-                XG, XR, DY, WV, WP, WO, WR, AS, AR, AO, DS, DR, DO, DB, HL, HP, DXS, DXA, DXM, DXF, DXR, XT,
+                XG, XR, DY, WV, WP, WO, WR, AS, AR, AO, DO, DB, HL, HP, DXS, DXA, DXM, DXF, DXR, XT,
                 send_ref, recv_ref, local_ref):
     fq = ff // 4
     cm = dm
@@ -53,7 +57,6 @@
     pr, c = z // 2, z % 2
     zm, zt = z + 1 - 2 * c, z + 2 - 4 * pr
     home, away = y == pr, y != pr
-    role = jnp.where(home, 0, 1)
     zeta = jnp.where(y == 0, z, 3 - z)
     zf, zb = z + 1 - 2 * y, z - 1 + 2 * y
     z2 = jnp.where(y == 0, 2, 1)
@@ -70,11 +73,11 @@
 
     pending = []
 
-    def remote(src, dst, name, to):
-        return pltpu.make_async_remote_copy(src_ref=src, dst_ref=dst, send_sem=S(*name), recv_sem=R(*name), device_id=to, device_id_type=MESH)
-
-    def send(src, dst, name, to, cond=None, last=None):
-        cp = remote(src, dst, name, to)
+    def remote(src, dst, name, to, off=None):
+        return pltpu.make_async_remote_copy(src_ref=src, dst_ref=dst, send_sem=S(*name), recv_sem=R(*name, off=off), device_id=to, device_id_type=MESH)
+
+    def send(src, dst, name, to, cond=None, last=None, off=None):
+        cp = remote(src, dst, name, to, off)
         if cond is None:
             cp.start()
         else:
@@ -82,8 +85,8 @@
         if last is not False:
             pending.append((cond if last is None else None if last is True else last, cp))
 
-    def got(dst, name, cond=None):
-        cp = remote(dst, dst, name, dev(p_=1 - p))
+    def got(dst, name, cond=None, off=None):
+        cp = remote(dst, dst, name, dev(p_=1 - p), off)
         if cond is None:
             cp.wait_recv()
         else:
@@ -93,18 +96,13 @@
         return pltpu.make_async_copy(src, dst, L(*name))
 
     barrier = pltpu.get_barrier_semaphore()
-    peers = [dev(r_=rp), dev(r_=ro), dev(r_=rx), dev(p_=1 - p), dev(z_=zt), dev(z_=zt + 1 - 2 * (zt % 2))]
-    peers += [dev(z_=zm, r_=q) for q in range(4)]
+    peers = [dev(p_=1 - p)] + [dev(z_=(z + dz) % 4, r_=(r + dr) % 4) for dz in range(4) for dr in range(4) if dz or dr]
     for peer in peers:
         pl.semaphore_signal(barrier, inc=1, device_id=peer, device_id_type=MESH)
 
-    @pl.when(jnp.logical_not(diag))
-    def _():
-        pl.semaphore_signal(barrier, inc=1, device_id=dev(z_=r, r_=z), device_id_type=MESH)
-
     lx = local(x_hbm, XG.at[c, k, y], "x")
     pl.when(home)(lx.start)
-    ldy = local(gy_hbm, DY.at[c, k, y], "dy")
+    ldy = local(gy_hbm, DY.at[z, k, y], "dy")
     ldy.start()
     lw = []
     for m, w in enumerate((wg_hbm, wu_hbm)):
@@ -113,23 +111,24 @@
             cp.start()
             lw.append(cp)
 
+    half = cm // 2
+    pcols = pl.ds(pl.multiple_of(p * half, 512), half)
+    line = (z, zm, zt, zt + 1 - 2 * (zt % 2))
+
     def wo_cut(q, n, cols):
         off, ln = N_CUT[n]
         return wo_hbm.at[pl.ds(pl.multiple_of(q * fq + off, 128), ln), cols]
 
-    def wo_slot(ro_, n, j, cols):
+    def wo_slot(n, src_z, start, width):
         off, ln = N_CUT[n]
-        start, width = cols
-        return WO.at[ro_, pl.ds(off, ln), pl.ds(pl.multiple_of(j * cm + start, 512), width)]
-
-    half = cm // 2
-    pcols = pl.ds(pl.multiple_of(p * half, 512), half)
+        return WO.at[pl.ds(off, ln), pl.ds(pl.multiple_of(src_z * cm + start, 512), width)]
+
     lwo = []
     for n in NS:
-        cp = local(wo_cut(r, n, pl.ds(0, cm)), wo_slot(role, n, c, (0, cm)), "wo", n)
-        pl.when(k == c)(cp.start)
+        cp = local(wo_cut(r, n, pl.ds(0, cm)), wo_slot(n, z, 0, cm), "wo", n)
+        pl.when(diag)(cp.start)
         lwo.append(cp)
-    pl.semaphore_wait(barrier, jnp.where(diag, len(peers), len(peers) + 1))
+    pl.semaphore_wait(barrier, len(peers))
 
     def chunk(t):
         return pl.ds(OFF[t], RBS[t])
@@ -171,83 +170,84 @@
     def x_take(th):
         got(XG.at[:, 1 - k, :, pl.ds(*X_CUT[th])], ("xd", th))
 
+    def dy_send():
+        send(gy_hbm, DY.at[z, k, y], ("dyy",), dev(r_=ro))
+
     def dy_pass():
         ldy.wait()
-        got(DY.at[c, k, 1 - y], ("dyy",))
-        send(DY.at[c, k], DY.at[c, k], ("dyz",), dev(z_=zm))
-        send(DY.at[c, k], DY.at[c, k], ("dyd", 0), dev(r_=rp))
-
-    def dy_give():
-        got(DY.at[1 - c, k], ("dyz",))
-        send(DY.at[1 - c, k], DY.at[1 - c, k], ("dyd", 1), dev(r_=rp))
+        mine = DY.at[z, k]
+        got(DY.at[z, k, 1 - y], ("dyy",))
+        send(mine, mine, ("dr", 1), dev(z_=z + 1), z < 3)
+        send(mine, mine, ("dl", 1), dev(z_=z - 1), z > 0)
+        send(mine, mine, ("dyd", 0, 0), dev(r_=rp))
+
+    def dy_from(d, left):
+        src_z = z + d if left else z - d
+        return src_z, src_z <= 3 if left else src_z >= 0
+
+    def dy_step(d, left):
+        src_z, here = dy_from(d, left)
+        to = z - 1 if left else z + 1
+        more = to >= 0 if left else to <= 3
+        name = "dl" if left else "dr"
+        theirs = DY.at[src_z, k]
+        got(theirs, (name, d), here)
+        if d < 3:
+            send(theirs, theirs, (name, d + 1), dev(z_=to), both(here, more))
+        send(theirs, theirs, ("dyd", d, left), dev(r_=rp), here)
 
     def dy_take():
-        for i, j in enumerate((c, 1 - c)):
-            got(DY.at[j, 1 - k], ("dyd", i))
-
-    def wo_near(n, cond):
-        send(wo_cut(rp, n, pl.ds(0, cm)), wo_slot(role, n, c, (0, cm)), ("wo", 0, n), dev(r_=rp), both(cond, k == c))
+        got(DY.at[z, 1 - k], ("dyd", 0, 0))
+        for d in range(1, 4):
+            for left in range(2):
+                src_z, here = dy_from(d, left)
+                got(DY.at[src_z, 1 - k], ("dyd", d, left), here)
+
+    def wo_near(n):
+        send(wo_cut(rp, n, pl.ds(0, cm)), wo_slot(n, z, 0, cm), ("wn", n), dev(r_=rp), diag)
+
+    def wo_own(n):
+        for k2 in range(2):
+            q = 2 * y + k2
+            send(wo_cut(q, n, pcols), wo_slot(n, z, p * half, half), ("wz", n, k2), dev(z_=r, r_=q), jnp.logical_not(diag), None, z)
+
+    def wo_cross(n):
+        off, ln = N_CUT[n]
         for k2 in range(2):
             q = 2 * (1 - y) + k2
-            send(wo_cut(q, n, pcols), wo_slot(role, n, c, (p * half, half)), ("wo", 1, n, k2), dev(r_=q), both(cond, k == c))
-
-    def wo_far(n, over, cond):
+            send(wo_cut(q, n, pcols), wo_slot(n, z, p * half, half), ("wd", n, k2), dev(r_=q), diag)
+            send(wo_cut(q, n, pcols), WR.at[k2, pl.ds(off, ln)], ("wr", n, k2), dev(r_=ro), jnp.logical_not(diag))
+
+    def wo_relay(n):
         off, ln = N_CUT[n]
         for k2 in range(2):
-            q = 2 * (1 - y if over else y) + k2
-            dst = WR.at[pl.ds(off, ln)] if over else wo_slot(role, n, c, (p * half, half))
-            send(wo_cut(q, n, pcols), dst, ("wf" if over else "wo", 2, n, k2), dev(z_=zm, r_=2 * y + k2), both(cond, k != c))
-
-    def wo_relay(n, cond):
+            got(WR.at[k2, pl.ds(off, ln)], ("wr", n, k2), z != ro)
+            send(WR.at[k2, pl.ds(off, ln)], wo_slot(n, z, p * half, half), ("wv", n, k2), dev(z_=ro, r_=2 * y + k2), z != ro, None, z)
+
+    def wo_pass(n, i):
+        src_z = line[i]
+        mine = wo_slot(n, src_z, p * half, half)
+        for k2 in range(2):
+            if i == 0:
+                got(mine, ("wd", n, k2), both(away, k == k2))
+            else:
+                got(mine, ("wz", n, k2), both(home, k == k2), src_z)
+                got(mine, ("wv", n, k2), both(away, k == k2), src_z)
+        send(mine, mine, ("wx", n, i), dev(p_=1 - p), away if i == 0 else None)
+
+    def dh_part(n):
         off, ln = N_CUT[n]
-        for k2 in range(2):
-            got(WR.at[pl.ds(off, ln)], ("wf", 2, n, k2), both(cond, k == k2))
-        send(WR.at[pl.ds(off, ln)], wo_slot(role, n, 1 - c, (p * half, half)), ("wo", 3, n), dev(r_=ro), cond)
-
-    def wo_role(a):
-        return jnp.where(home, a % 2, 1 - a % 2)
-
-    def wo_pass(a, n, cond):
-        j = c if a == 1 else 1 - c
-        mine = wo_slot(wo_role(a), n, j, (p * half, half))
-        if a == 3:
-            got(mine, ("wo", a, n), cond)
-        else:
-            for k2 in range(2):
-                got(mine, ("wo", a, n, k2), both(cond, k == k2))
-        send(mine, mine, ("wx", a, n), dev(p_=1 - p), cond)
-
-    def wo_have(a, n, cond):
-        j = c if a < 2 else 1 - c
-        if a == 0:
-            pl.when(both(cond, k == c))(lwo[n].wait)
-            got(wo_slot(wo_role(a), n, j, (0, cm)), ("wo", 0, n), both(cond, k != c))
-        else:
-            got(wo_slot(wo_role(a), n, j, ((1 - p) * half, half)), ("wx", a, n), cond)
-
-    def dh_part(ro_, n, dst):
-        off, ln = N_CUT[n]
-        acc = None
-        for j in range(2):
-            t = lax.dot_general(DY[j].reshape(4 * rows, cm), WO[ro_, off:off + ln, j * cm:(j + 1) * cm], NT_DIMS, preferred_element_type=F32)
-            acc = t if acc is None else acc + t
-        dst[:, :, off:off + ln] = acc.reshape(4, rows, ln)
-
-    def dh_cols(n, t):
-        off, ln = N_CUT[n]
-        return slice(None), chunk(t) if n == NS[-1] else pl.ds(0, rows), pl.ds(off, ln)
-
-    def dh_mirror(n):
-        for a in range(4):
-            wo_have(a, n, home if a % 2 else away)
-        dh_part(1, n, DS)
-        for t in range(NCH if n == NS[-1] else 1):
-            send(DS.at[dh_cols(n, t)], DR.at[dh_cols(n, t)], ("dh", n, t), dev(z_=zt))
-
-    def dh_own(n):
-        for a in range(4):
-            wo_have(a, n, away if a % 2 else home)
-        dh_part(0, n, DO)
+        pl.when(both(home, diag))(lwo[n].wait)
+        got(wo_slot(n, z, 0, cm), ("wn", n), both(home, jnp.logical_not(diag)))
+        for i in range(4):
+            got(wo_slot(n, line[i], (1 - p) * half, half), ("wx", n, i), away if i == 0 else None)
+
+        def go():
+            for j in range(4):
+                d = lax.dot_general(DY[j].reshape(4 * rows, cm), WO[off:off + ln, j * cm:(j + 1) * cm], NT_DIMS, preferred_element_type=F32).reshape(4, rows, ln)
+                DO[:, :, off:off + ln] = d if j == 0 else DO[:, :, off:off + ln] + d
+
+        go()
 
     def ab_part(s, t):
         tc = 4 * RBS[t]
@@ -300,12 +300,8 @@
         send(HL.at[2, y, :, chunk(t)], HL.at[c, y, :, chunk(t)], ("hy", t), dev(r_=ro), away)
 
     def finish_dh(t):
-        for n in NS:
-            if n == NS[-1] or t == 0:
-                got(DR.at[dh_cols(n, t)], ("dh", n, t))
-
         def body(o, rs):
-            dh = DO[o, rs] + DR[o, rs]
+            dh = DO[o, rs]
             DB[r, o, rs, :fq] = (dh * AR[o, rs, :fq]).astype(BF16)
             DB[r, o, rs, fq:] = (dh * AR[o, rs, fq:]).astype(BF16)
 
@@ -354,8 +350,10 @@
     target = jnp.where(y == 0, k, 1 - k)
 
     def piece(u):
-        t, ln = u // 2, RBS[u // 2] // 2
-        return OFF[t] + u % 2 * ln, ln
+        return PIECES[u][1:]
+
+    def pieces(t):
+        return [u for u in range(len(PIECES)) if PIECES[u][0] == t]
 
     def dx_part(t, i):
         q = (r, rp, ro, rx)[i]
@@ -375,7 +373,7 @@
         if i < 3:
             return
         if t < CHAIN:
-            for u in (2 * t, 2 * t + 1):
+            for u in pieces(t):
                 rs = pl.ds(*piece(u))
                 send(DXS.at[:, :, rs], DXA.at[:, :, rs], ("dxa", u), dev(z_=zb), zeta == 3, False)
                 send(DXS.at[:, :, rs], DXM.at[:, :, rs], ("dxm", u), dev(z_=zf), both(zeta == 0, target == 1))
@@ -437,9 +435,6 @@
         go()
         send(DXF.at[k, y, chunk(t)], DXR.at[chunk(t)], ("dxt", t), dev(z_=r, r_=z), jnp.logical_not(diag))
 
-    def dy_send():
-        send(gy_hbm, DY.at[c, k, y], ("dyy",), dev(r_=ro))
-
     def w_swap():
         for m, w in enumerate((wg_hbm, wu_hbm)):
             for s in range(2):
@@ -458,7 +453,7 @@
             DXR.__setitem__(sl, DXF[k, y, sl])
 
         if t < CHAIN:
-            for u in (2 * t, 2 * t + 1):
+            for u in pieces(t):
                 rs = pl.ds(*piece(u))
                 got(DXR.at[rs], ("dxf", u, 0), both(zk != k, zy == y))
                 got(DXR.at[rs], ("dxf", u, 1), both(zk == k, zy != y))
@@ -469,169 +464,144 @@
     def out_early():
         XT.__setitem__(Ellipsis, XG[k].reshape(4 * rows, cm).T)
         out(XT, xo, "xo")
-        out(DY.at[c], dyo, "dyo")
+        out(DY.at[z], dyo, "dyo")
 
     i0, i1, i2, i3, i4, i5, i6, i7, i8, i9 = range(10)
     yes, no = True, False
-    wo_near(i1, home)
-    wo_far(i0, i1, home)
     x_send(i0)
-    wo_near(i2, home)
-    wo_far(i1, i0, home)
     dy_send()
-    wo_far(i2, i1, home)
-    wo_far(i0, i1, away)
-    wo_relay(i0, home)
+    wo_cross(i1)
+    wo_cross(i0)
     x_send(i1)
-    wo_near(i0, away)
-    wo_far(i1, i1, away)
-    w_swap()
-    wo_pass(i2, i1, home)
     x_step(i0, i1, i1)
-    wo_relay(i2, home)
     x_step(i0, i1, i0)
     x_step(i1, i1, i1)
+    x_step(i0, i2, i0)
+    x_step(i0, i3, i0)
     x_step(i1, i1, i0)
-    wo_near(i1, away)
-    wo_pass(i3, i0, away)
-    wo_far(i0, i0, away)
     x_step(i0, i2, i1)
+    dy_pass()
+    x_step(i1, i2, i0)
+    wo_own(i1)
+    wo_near(i1)
+    w_swap()
+    wo_relay(i1)
+    x_step(i0, i3, i1)
+    x_step(i1, i2, i1)
+    x_give(i0)
+    x_step(i1, i3, i1)
+    dy_step(i1, i1)
+    wo_near(i0)
+    dy_step(i1, i0)
+    wo_own(i0)
+    wo_pass(i0, i0)
+    wo_relay(i0)
+    x_step(i1, i3, i0)
     weights_here()
-    wo_far(i0, i0, home)
-    x_step(i0, i2, i0)
-    wo_relay(i0, away)
-    x_step(i1, i2, i0)
-    x_step(i1, i2, i1)
-    dy_pass()
-    wo_far(i2, i0, home)
-    x_step(i0, i3, i0)
-    wo_far(i1, i1, home)
-    wo_pass(i1, i0, home)
-    wo_far(i1, i0, away)
-    wo_near(i0, home)
-    wo_near(i2, away)
-    x_step(i1, i3, i0)
-    wo_pass(i1, i1, home)
-    wo_pass(i3, i0, home)
-    wo_pass(i2, i0, home)
-    wo_pass(i1, i2, away)
-    wo_relay(i1, away)
-    x_step(i0, i3, i1)
-    x_give(i0)
     x_take(i0)
-    x_step(i1, i3, i1)
-    wo_pass(i1, i1, away)
+    ab_mirror(i0, home, yes)
     ab_mirror(i1)
+    wo_pass(i1, i0)
+    ab_mirror(i0, away, no)
     x_give(i1)
     x_take(i1)
     ab_mirror(i2)
-    ab_mirror(i0, home, yes)
-    wo_pass(i1, i0, away)
-    wo_far(i2, i0, away)
-    wo_pass(i2, i0, away)
-    dy_give()
-    wo_pass(i3, i1, home)
-    wo_far(i2, i1, away)
+    wo_pass(i1, i1)
+    wo_pass(i1, i3)
+    wo_pass(i1, i2)
+    finish_ab(i0)
+    dy_step(i2, i1)
+    finish_ab(i1)
+    wo_pass(i0, i1)
+    dy_step(i2, i0)
+    wo_pass(i0, i3)
+    finish_ab(i2)
+    ab_mirror(i3)
+    h_start(i0)
+    wo_pass(i0, i2)
+    dy_step(i3, i0)
+    h_start(i1)
+    dy_step(i3, i1)
+    h_start(i2)
     dy_take()
-    dh_mirror(i0)
-    wo_pass(i1, i2, home)
-    wo_pass(i2, i1, away)
-    dh_mirror(i1)
-    wo_relay(i1, home)
-    wo_relay(i2, away)
-    wo_pass(i2, i2, away)
-    finish_ab(i2)
-    wo_pass(i3, i2, home)
-    h_start(i2)
-    dh_own(i0)
-    wo_pass(i3, i2, away)
-    dh_mirror(i2)
-    ab_mirror(i0, away, no)
-    finish_ab(i1)
-    wo_pass(i2, i2, home)
-    ab_mirror(i3)
+    dh_part(i1)
+    dh_part(i0)
+    finish_dh(i0)
+    finish_dh(i2)
+    h_pass(i0, i0)
+    h_pass(i0, i1)
+    h_pass(i2, i1)
+    finish_ab(i3)
+    dx_part(i0, i0)
+    finish_dh(i1)
+    dx_part(i0, i1)
+    dx_part(i1, i0)
+    finish_dh(i3)
+    h_pass(i1, i0)
+    dx_part(i2, i0)
+    relay_db(i0)
+    dx_part(i0, i2)
+    h_pass(i2, i0)
+    dx_part(i2, i1)
+    dx_part(i0, i3)
+    dx_part(i3, i0)
+    h_pass(i0, i2)
+    h_pass(i1, i1)
+    relay_db(i2)
+    dx_part(i2, i2)
+    dx_step(i0, i2)
+    dx_part(i2, i3)
+    h_start(i3)
+    dx_part(i1, i1)
+    dx_step(i0, i1)
+    dx_step(i1, i2)
+    relay_db(i1)
+    dx_part(i1, i2)
+    h_pass(i2, i2)
+    dx_part(i1, i3)
+    dx_step(i1, i1)
+    dx_step(i4, i2)
+    dx_step(i4, i1)
+    dx_part(i3, i1)
+    h_pass(i1, i2)
+    relay_db(i3)
+    dx_part(i3, i2)
+    dx_step(i0, i0)
+    dx_step(i5, i2)
+    dx_spread(i0)
+    h_pass(i3, i0)
+    dx_part(i3, i3)
+    h_pass(i3, i1)
     out_early()
-    dh_own(i2)
-    wo_pass(i3, i1, away)
-    finish_ab(i0)
-    dh_own(i1)
-    finish_dh(i0)
-    finish_dh(i1)
-    h_start(i1)
-    finish_ab(i3)
-    dx_part(i1, i0)
-    dx_part(i0, i0)
-    h_start(i0)
-    h_pass(i2, i0)
-    finish_dh(i2)
-    relay_db(i0)
-    dx_part(i0, i1)
-    finish_dh(i3)
-    h_pass(i2, i1)
-    dx_part(i0, i2)
-    dx_part(i0, i3)
-    dx_part(i1, i1)
-    relay_db(i1)
-    h_pass(i1, i0)
-    h_start(i3)
-    dx_part(i1, i2)
-    dx_part(i1, i3)
-    dx_part(i2, i0)
-    h_pass(i0, i1)
-    dx_step(i0, i2)
-    h_pass(i0, i0)
-    dx_part(i2, i1)
-    relay_db(i2)
-    h_pass(i1, i1)
-    dx_part(i2, i2)
-    dx_part(i3, i0)
-    dx_step(i1, i2)
-    dx_step(i0, i1)
-    dx_part(i2, i3)
-    dx_step(i1, i1)
-    relay_db(i3)
-    dx_step(i0, i0)
-    h_pass(i2, i2)
-    dx_part(i3, i1)
+    dx_step(i4, i0)
+    dx_step(i5, i1)
+    h_last(i1)
+    dx_spread(i4)
     dx_step(i2, i2)
+    dx_step(i1, i0)
+    h_last(i0)
+    dx_step(i5, i0)
+    dx_step(i3, i2)
+    dx_spread(i1)
     dx_step(i2, i1)
-    dx_part(i3, i2)
-    dx_part(i3, i3)
+    h_take(i1)
+    dx_half(i3)
+    dx_step(i3, i1)
+    h_last(i2)
     dx_step(i2, i0)
-    h_pass(i3, i0)
     dx_spread(i2)
-    dx_step(i3, i2)
-    dx_step(i3, i1)
-    dx_step(i1, i0)
-    h_pass(i0, i2)
-    h_pass(i3, i1)
-    dx_step(i4, i2)
-    dx_step(i5, i2)
+    h_pass(i3, i2)
+    dx_spread(i5)
     dx_step(i3, i0)
-    dx_step(i4, i1)
-    dx_spread(i1)
-    dx_half(i3)
-    dx_step(i4, i0)
-    h_last(i2)
-    dx_spread(i0)
     dx_spread(i3)
-    dx_spread(i4)
-    dx_step(i5, i1)
-    dx_step(i5, i0)
-    h_last(i0)
-    dx_spread(i5)
-    h_pass(i1, i2)
+    h_take(i2)
+    h_take(i0)
     dx_quarter(i3)
-    h_pass(i3, i2)
-    h_last(i1)
+    dx_take(i0)
+    h_last(i3)
+    dx_take(i2)
     dx_take(i1)
-    dx_take(i2)
-    h_take(i0)
-    h_take(i1)
-    h_take(i2)
     dx_take(i3)
-    h_last(i3)
-    dx_take(i0)
     h_take(i3)
 
     out(DXR, dxo, "dxo")
@@ -698,16 +668,14 @@
             scratch_shapes=[
                 vm((2, 2, 2, rows, dm), BF16),
                 vm((2, rows, dm), BF16),
-                vm((2, 2, 2, rows, dm), BF16),
+                vm((4, 2, 2, rows, dm), BF16),
                 vm((4, dm, 2 * fq), BF16),
                 vm((2, dm, 2 * fq), BF16),
-                vm((2, fq, 2 * dm), BF16),
-                vm((fq, dm // 2), BF16),
+                vm((fq, 4 * dm), BF16),
+                vm((2, fq, dm // 2), BF16),
                 vm((4, rows, 2 * fq), F32),
                 vm((4, rows, 2 * fq), F32),
                 vm((4, max(RBS), 2 * fq), F32),
-                vm((4, rows, fq), F32),
-                vm((4, rows, fq), F32),
                 vm((4, rows, fq), F32),
                 vm((4, 4, rows, 2 * fq), BF16),
                 vm((3, 2, 4, rows, fq), BF16),

time: 203 us -> 200 us (0.985)
  Pallas kernels: 200 us -> 197 us
    pallas_call x1, Pallas kernels: 184 us -> 181 us  [block_backward(): pl.pallas_call(lambda *refs: comm_kernel(rows, dm, ff, *refs), out_shape=...]
where the time goes in v5:
time: 200 us; the launch traced here: 198 us
  Pallas kernels  197 us (98%)
    pallas_call x1, Pallas kernels, block_backward(): pl.pallas_call(lambda *refs: comm_kernel(rows, dm, ff, *refs), out_shape=...  181 us
    pallas_call x1, Pallas kernels, block_backward(): pl.pallas_call(dw_kernel, out_shape=[jax.ShapeDtypeStruct((dm, ff), F32),...  16.1 us

profile of v5, /device:TPU:0, one launch (start us, length us, event | category | flops | bytes accessed | tf_op | source)
XLA Modules:
  0.0 198.2 jit_solution(11517285592923167286)
XLA Ops:
  0.6 181.3 %comm.1 = (bf16[1024,512]{1,0:T(8,128)(2,1)}, bf16[2,2,128,1024]{3,2,1,0:T(8,128)(2,1)}, bf16[4,4,128,1280]{3,2,1,0:T(8,128)(2,1)}, bf16[2,2,4,128,640]{4,3,2,1,0:T(8,128)(2,1)}, bf16[128,1024]{1,0:T(8,128)(2,1)}) custom-call(bf16[128,1024]{1,0:T(8,128)(2,1)} %refs_0_.1, bf16[128,1024]{1,0:T(8,128)(2,1)} %refs_1_.1, bf16[1024,2560]{1,0:T(8,128)(2,1)} %refs_2_.1, ...), custom_call_target="tpu_custom_call" | custom-call | tf_op jit(solution)/shard_map/comm/pallas_call | solution.py:657
  181.9 16.1 %dw.1 = (f32[1024,2560]{1,0:T(8,128)}, f32[1024,2560]{1,0:T(8,128)}, f32[2560,1024]{1,0:T(8,128)}, bf16[128,1024]{1,0:T(8,128)(2,1)}) custom-call(bf16[1024,512]{1,0:T(8,128)(2,1)} %get-tuple-element.13.x_hbm, bf16[512,1024]{1,0:T(8,128)(2,1)} %bitcast.5, bf16[4,512,1280]{2,1,0:T(8,128)(2,1)} %bitcast.3, bf16[4,512,640]{2,1,0:T(8,128)(2,1)} %bitcast.4, ...), custom_call_target="tpu_custom_call" | custom-call | tf_op jit(solution)/shard_map/dw/pallas_call | solution.py:697

commit v6 on v5

--- a/solution.py
+++ b/solution.py
@@ -470,136 +470,136 @@
     yes, no = True, False
     x_send(i0)
     dy_send()
+    w_swap()
     wo_cross(i1)
+    x_send(i1)
+    x_step(i0, i1, i0)
+    x_step(i0, i1, i1)
+    x_step(i0, i2, i1)
+    x_step(i1, i1, i1)
+    wo_near(i1)
+    x_step(i0, i2, i0)
+    x_step(i1, i1, i0)
+    dy_pass()
+    x_step(i0, i3, i0)
     wo_cross(i0)
-    x_send(i1)
-    x_step(i0, i1, i1)
-    x_step(i0, i1, i0)
-    x_step(i1, i1, i1)
-    x_step(i0, i2, i0)
-    x_step(i0, i3, i0)
-    x_step(i1, i1, i0)
-    x_step(i0, i2, i1)
-    dy_pass()
     x_step(i1, i2, i0)
+    x_step(i0, i3, i1)
+    x_step(i1, i3, i0)
+    x_step(i1, i2, i1)
+    wo_near(i0)
+    weights_here()
+    wo_relay(i1)
     wo_own(i1)
-    wo_near(i1)
-    w_swap()
-    wo_relay(i1)
-    x_step(i0, i3, i1)
-    x_step(i1, i2, i1)
     x_give(i0)
+    dy_step(i1, i0)
     x_step(i1, i3, i1)
-    dy_step(i1, i1)
-    wo_near(i0)
-    dy_step(i1, i0)
-    wo_own(i0)
-    wo_pass(i0, i0)
-    wo_relay(i0)
-    x_step(i1, i3, i0)
-    weights_here()
     x_take(i0)
     ab_mirror(i0, home, yes)
+    dy_step(i1, i1)
     ab_mirror(i1)
     wo_pass(i1, i0)
+    x_give(i1)
+    wo_own(i0)
     ab_mirror(i0, away, no)
-    x_give(i1)
+    wo_pass(i0, i0)
     x_take(i1)
     ab_mirror(i2)
+    wo_pass(i1, i2)
+    wo_pass(i1, i3)
+    wo_relay(i0)
     wo_pass(i1, i1)
-    wo_pass(i1, i3)
-    wo_pass(i1, i2)
     finish_ab(i0)
+    finish_ab(i1)
     dy_step(i2, i1)
-    finish_ab(i1)
+    ab_mirror(i3)
+    dy_step(i2, i0)
     wo_pass(i0, i1)
-    dy_step(i2, i0)
     wo_pass(i0, i3)
-    finish_ab(i2)
-    ab_mirror(i3)
-    h_start(i0)
     wo_pass(i0, i2)
     dy_step(i3, i0)
+    finish_ab(i2)
+    h_start(i0)
+    dy_step(i3, i1)
     h_start(i1)
-    dy_step(i3, i1)
-    h_start(i2)
     dy_take()
     dh_part(i1)
     dh_part(i0)
+    h_pass(i0, i0)
     finish_dh(i0)
+    h_pass(i0, i1)
+    finish_ab(i3)
     finish_dh(i2)
-    h_pass(i0, i0)
-    h_pass(i0, i1)
+    dx_part(i2, i0)
+    finish_dh(i1)
+    dx_part(i0, i0)
+    finish_dh(i3)
+    dx_part(i3, i0)
+    dx_part(i1, i0)
+    h_start(i2)
+    h_pass(i1, i0)
+    dx_part(i0, i1)
+    relay_db(i0)
+    h_start(i3)
+    dx_part(i0, i2)
+    dx_part(i0, i3)
+    h_pass(i0, i2)
     h_pass(i2, i1)
-    finish_ab(i3)
-    dx_part(i0, i0)
-    finish_dh(i1)
-    dx_part(i0, i1)
-    dx_part(i1, i0)
-    finish_dh(i3)
-    h_pass(i1, i0)
-    dx_part(i2, i0)
-    relay_db(i0)
-    dx_part(i0, i2)
-    h_pass(i2, i0)
     dx_part(i2, i1)
-    dx_part(i0, i3)
-    dx_part(i3, i0)
-    h_pass(i0, i2)
-    h_pass(i1, i1)
+    dx_part(i3, i1)
     relay_db(i2)
     dx_part(i2, i2)
+    dx_part(i1, i1)
+    dx_part(i2, i3)
+    h_pass(i2, i0)
+    h_last(i0)
     dx_step(i0, i2)
-    dx_part(i2, i3)
-    h_start(i3)
-    dx_part(i1, i1)
-    dx_step(i0, i1)
     dx_step(i1, i2)
     relay_db(i1)
+    h_pass(i3, i0)
+    dx_step(i1, i1)
     dx_part(i1, i2)
+    dx_part(i1, i3)
+    dx_step(i0, i1)
+    h_pass(i1, i1)
+    dx_step(i4, i2)
+    h_pass(i3, i1)
+    relay_db(i3)
     h_pass(i2, i2)
-    dx_part(i1, i3)
-    dx_step(i1, i1)
-    dx_step(i4, i2)
     dx_step(i4, i1)
-    dx_part(i3, i1)
-    h_pass(i1, i2)
-    relay_db(i3)
+    dx_step(i5, i2)
     dx_part(i3, i2)
-    dx_step(i0, i0)
-    dx_step(i5, i2)
-    dx_spread(i0)
-    h_pass(i3, i0)
+    dx_step(i1, i0)
+    dx_step(i4, i0)
     dx_part(i3, i3)
-    h_pass(i3, i1)
-    out_early()
-    dx_step(i4, i0)
     dx_step(i5, i1)
-    h_last(i1)
     dx_spread(i4)
     dx_step(i2, i2)
-    dx_step(i1, i0)
-    h_last(i0)
+    dx_spread(i1)
+    h_pass(i1, i2)
     dx_step(i5, i0)
+    out_early()
+    h_take(i0)
     dx_step(i3, i2)
-    dx_spread(i1)
     dx_step(i2, i1)
-    h_take(i1)
+    dx_spread(i5)
+    h_last(i1)
     dx_half(i3)
+    dx_step(i2, i0)
+    h_last(i2)
+    dx_spread(i2)
+    dx_step(i0, i0)
+    dx_spread(i0)
     dx_step(i3, i1)
-    h_last(i2)
-    dx_step(i2, i0)
-    dx_spread(i2)
-    h_pass(i3, i2)
-    dx_spread(i5)
+    h_take(i2)
     dx_step(i3, i0)
     dx_spread(i3)
-    h_take(i2)
-    h_take(i0)
+    h_take(i1)
+    dx_take(i2)
+    h_pass(i3, i2)
     dx_quarter(i3)
+    h_last(i3)
     dx_take(i0)
-    h_last(i3)
-    dx_take(i2)
     dx_take(i1)
     dx_take(i3)
     h_take(i3)
@@ -614,12 +614,13 @@
         cp.wait()
 
 
-def dw_kernel(x_hbm, dy_hbm, db_hbm, h_hbm, dx_hbm, dwg, dwu, dwo, dxo, XT, DY, DB, H, OA, OB, in_sem, out_sem):
+def dw_kernel(x_hbm, dy_hbm, db_hbm, h_hbm, dx_hbm, dwg, dwu, dwo, dxo, XT, DY, DB, H, DX, OA, OB, in_sem, out_sem):
     fq = H.shape[-1]
     loads = [pltpu.make_async_copy(x_hbm, XT, in_sem.at[0])]
     loads += [pltpu.make_async_copy(db_hbm.at[q], DB.at[q], in_sem.at[1 + q]) for q in range(4)]
     loads += [pltpu.make_async_copy(dy_hbm, DY, in_sem.at[5])]
     loads += [pltpu.make_async_copy(h_hbm.at[q], H.at[q], in_sem.at[6 + q]) for q in range(4)]
+    loads += [pltpu.make_async_copy(dx_hbm, DX, in_sem.at[10])]
     for cp in loads:
         cp.start()
     outs = []
@@ -635,12 +636,13 @@
         OA[q] = jnp.dot(XT[...], DB[q], preferred_element_type=F32)
         for m, dst in enumerate((dwg, dwu)):
             put(OA.at[q, :, pl.ds(m * fq, fq)], dst.at[:, pl.ds(q * fq, fq)])
+    loads[10].wait()
+    put(DX, dxo)
     loads[5].wait()
     for q in range(4):
         loads[6 + q].wait()
         OB[q] = lax.dot_general(H[q], DY[...], TN_DIMS, preferred_element_type=F32)
         put(OB.at[q], dwo.at[pl.ds(q * fq, fq)])
-    dxo[...] = dx_hbm[...]
     for cp in outs:
         cp.wait()
 
@@ -693,7 +695,6 @@
             compiler_params=pltpu.CompilerParams(collective_id=0, has_side_effects=True, vmem_limit_bytes=63 * 1024 * 1024),
             name="comm",
         )(x_blk, gy_blk, gate_blk, up_blk, out_blk)
-        whole = pl.BlockSpec(memory_space=vm)
         dw_gate, dw_up, dw_out, grad_x = pl.pallas_call(
             dw_kernel,
             out_shape=[
@@ -702,13 +703,13 @@
                 jax.ShapeDtypeStruct((ff, dm), F32),
                 jax.ShapeDtypeStruct((rows, dm), BF16),
             ],
-            in_specs=[ANY] * 4 + [whole],
-            out_specs=[ANY] * 3 + [whole],
+            in_specs=[ANY] * 5,
+            out_specs=[ANY] * 4,
             scratch_shapes=[
                 vm((dm, tok), BF16), vm((tok, dm), BF16),
-                vm((4, tok, 2 * fq), BF16), vm((4, tok, fq), BF16),
+                vm((4, tok, 2 * fq), BF16), vm((4, tok, fq), BF16), vm((rows, dm), BF16),
                 vm((4, dm, 2 * fq), F32), vm((4, fq, dm), F32),
-                pltpu.SemaphoreType.DMA((10,)), pltpu.SemaphoreType.DMA((12,)),
+                pltpu.SemaphoreType.DMA((11,)), pltpu.SemaphoreType.DMA((13,)),
             ],
             compiler_params=pltpu.CompilerParams(vmem_limit_bytes=60 * 1024 * 1024),
             name="dw",

time: 200 us -> 198 us (0.990)
  no operation moved by 1% of the time
where the time goes in v6:
time: 198 us
  Pallas kernels  197 us (99%)
    pallas_call x1, Pallas kernels, block_backward(): pl.pallas_call(lambda *refs: comm_kernel(rows, dm, ff, *refs), out_shape=...  182 us
    pallas_call x1, Pallas kernels, block_backward(): pl.pallas_call(dw_kernel, out_shape=[jax.ShapeDtypeStruct((dm, ff), F32),...  14.5 us

profile of v6, /device:TPU:0, one launch (start us, length us, event | category | flops | bytes accessed | tf_op | source)
XLA Modules:
  0.0 197.6 jit_solution(12361892118039643013)
XLA Ops:
  0.6 182.3 %comm.1 = (bf16[1024,512]{1,0:T(8,128)(2,1)}, bf16[2,2,128,1024]{3,2,1,0:T(8,128)(2,1)}, bf16[4,4,128,1280]{3,2,1,0:T(8,128)(2,1)}, bf16[2,2,4,128,640]{4,3,2,1,0:T(8,128)(2,1)}, bf16[128,1024]{1,0:T(8,128)(2,1)}) custom-call(bf16[128,1024]{1,0:T(8,128)(2,1)} %refs_0_.1, bf16[128,1024]{1,0:T(8,128)(2,1)} %refs_1_.1, bf16[1024,2560]{1,0:T(8,128)(2,1)} %refs_2_.1, ...), custom_call_target="tpu_custom_call" | custom-call | tf_op jit(solution)/shard_map/comm/pallas_call | solution.py:659
  182.9 14.5 %dw.1 = (f32[1024,2560]{1,0:T(8,128)}, f32[1024,2560]{1,0:T(8,128)}, f32[2560,1024]{1,0:T(8,128)}, bf16[128,1024]{1,0:T(8,128)(2,1)}) custom-call(bf16[1024,512]{1,0:T(8,128)(2,1)} %get-tuple-element.13.x_hbm, bf16[512,1024]{1,0:T(8,128)(2,1)} %bitcast.5, bf16[4,512,1280]{2,1,0:T(8,128)(2,1)} %bitcast.3, bf16[4,512,640]{2,1,0:T(8,128)(2,1)} %bitcast.4, ...), custom_call_target="tpu_custom_call" | custom-call | tf_op jit(solution)/shard_map/dw/pallas_call | solution.py:698

commit v7 on v6

--- a/solution.py
+++ b/solution.py
@@ -96,9 +96,14 @@
         return pltpu.make_async_copy(src, dst, L(*name))
 
     barrier = pltpu.get_barrier_semaphore()
-    peers = [dev(p_=1 - p)] + [dev(z_=(z + dz) % 4, r_=(r + dr) % 4) for dz in range(4) for dr in range(4) if dz or dr]
+    peers = [dev(p_=1 - p), dev(r_=ro), dev(r_=rx)]
+    peers += [dev(z_=(z + dz) % 4, r_=2 * y + (k + dk) % 2) for dz in range(4) for dk in range(2) if dz or dk]
     for peer in peers:
         pl.semaphore_signal(barrier, inc=1, device_id=peer, device_id_type=MESH)
+
+    @pl.when(jnp.logical_not(diag))
+    def _():
+        pl.semaphore_signal(barrier, inc=1, device_id=dev(z_=r, r_=z), device_id_type=MESH)
 
     lx = local(x_hbm, XG.at[c, k, y], "x")
     pl.when(home)(lx.start)
@@ -128,7 +133,7 @@
         cp = local(wo_cut(r, n, pl.ds(0, cm)), wo_slot(n, z, 0, cm), "wo", n)
         pl.when(diag)(cp.start)
         lwo.append(cp)
-    pl.semaphore_wait(barrier, len(peers))
+    pl.semaphore_wait(barrier, jnp.where(diag, len(peers), len(peers) + 1))
 
     def chunk(t):
         return pl.ds(OFF[t], RBS[t])

time: 198 us -> 196 us (0.990)
  Pallas kernels: 197 us -> 195 us
    pallas_call x1, Pallas kernels: 182 us -> 180 us  [block_backward(): pl.pallas_call(lambda *refs: comm_kernel(rows, dm, ff, *refs), out_shape=...]
where the time goes in v7:
time: 196 us; the launch traced here: 195 us
  Pallas kernels  195 us (99%)
    pallas_call x1, Pallas kernels, block_backward(): pl.pallas_call(lambda *refs: comm_kernel(rows, dm, ff, *refs), out_shape=...  180 us
    pallas_call x1, Pallas kernels, block_backward(): pl.pallas_call(dw_kernel, out_shape=[jax.ShapeDtypeStruct((dm, ff), F32),...  14.5 us

profile of v7, /device:TPU:0, one launch (start us, length us, event | category | flops | bytes accessed | tf_op | source)
XLA Modules:
  0.0 195.5 jit_solution(13247057638447393427)
XLA Ops:
  0.6 180.2 %comm.1 = (bf16[1024,512]{1,0:T(8,128)(2,1)}, bf16[2,2,128,1024]{3,2,1,0:T(8,128)(2,1)}, bf16[4,4,128,1280]{3,2,1,0:T(8,128)(2,1)}, bf16[2,2,4,128,640]{4,3,2,1,0:T(8,128)(2,1)}, bf16[128,1024]{1,0:T(8,128)(2,1)}) custom-call(bf16[128,1024]{1,0:T(8,128)(2,1)} %refs_0_.1, bf16[128,1024]{1,0:T(8,128)(2,1)} %refs_1_.1, bf16[1024,2560]{1,0:T(8,128)(2,1)} %refs_2_.1, ...), custom_call_target="tpu_custom_call" | custom-call | tf_op jit(solution)/shard_map/comm/pallas_call | solution.py:664
  180.8 14.5 %dw.1 = (f32[1024,2560]{1,0:T(8,128)}, f32[1024,2560]{1,0:T(8,128)}, f32[2560,1024]{1,0:T(8,128)}, bf16[128,1024]{1,0:T(8,128)(2,1)}) custom-call(bf16[1024,512]{1,0:T(8,128)(2,1)} %get-tuple-element.13.x_hbm, bf16[512,1024]{1,0:T(8,128)(2,1)} %bitcast.5, bf16[4,512,1280]{2,1,0:T(8,128)(2,1)} %bitcast.3, bf16[4,512,640]{2,1,0:T(8,128)(2,1)} %bitcast.4, ...), custom_call_target="tpu_custom_call" | custom-call | tf_op jit(solution)/shard_map/dw/pallas_call | solution.py:703
